TPU v7x, 32 devices: a whole 2x2x4 slice. The times are simulated.
32 devices in a mesh: gz: 8 (over z, x), gy: 4 (over y, core).
Axes of the slice: x: 2, y: 2, z: 4, core: 2. Of those that a mesh axis runs over, the one named last changes fastest.
Arguments:
- source_first: float32 [64, 32, 16, 128], P('gz', 'gy'), may hold values from -6 to 6
- source_second: float32 [32, 16, 16, 128], P('gz', 'gy'), may hold values from -6 to 6
- source_third: float32 [16, 8, 16, 128], P('gz', 'gy'), may hold values from -6 to 6
- source_fourth: float32 [8, 4, 16, 128], P('gz', 'gy'), may hold values from -6 to 6
- guess_first: float32 [64, 32, 16, 128], P('gz', 'gy'), may hold values from -6 to 6
- guess_second: float32 [32, 16, 16, 128], P('gz', 'gy'), may hold values from -6 to 6
- guess_third: float32 [16, 8, 16, 128], P('gz', 'gy'), may hold values from -6 to 6
- guess_fourth: float32 [8, 4, 16, 128], P('gz', 'gy'), may hold values from -6 to 6
- shift_first: float32 [64, 32, 128], P('gz', 'gy'), may hold values from 0.2 to 2
- shift_second: float32 [32, 16, 128], P('gz', 'gy'), may hold values from 0.2 to 2
- shift_third: float32 [16, 8, 128], P('gz', 'gy'), may hold values from 0.2 to 2
- shift_fourth: float32 [8, 4, 128], P('gz', 'gy'), may hold values from 0.2 to 2
- blocks_first: bfloat16 [64, 32, 2, 128, 128], P('gz', 'gy'), may hold values from -0.375 to 0.375
- blocks_second: bfloat16 [32, 16, 2, 128, 128], P('gz', 'gy'), may hold values from -0.375 to 0.375
- blocks_third: bfloat16 [16, 8, 2, 128, 128], P('gz', 'gy'), may hold values from -0.375 to 0.375
- links_first: int32 [64, 32, 2], P('gz', 'gy'), may hold values from 0 to 511, as said below
- links_second: int32 [32, 16, 2], P('gz', 'gy'), may hold values from 0 to 127, as said below
- links_third: int32 [16, 8, 2], P('gz', 'gy'), may hold values from 0 to 31, as said below
Outputs:
- smooth_first: float32 [64, 32, 16, 128], P('gz', 'gy')
- smooth_second: float32 [32, 16, 16, 128], P('gz', 'gy')
- smooth_third: float32 [16, 8, 16, 128], P('gz', 'gy')
- smooth_fourth: float32 [8, 4, 16, 128], P('gz', 'gy')
Inputs may be any that keep to these rules, and one draw needn't show every extreme that they name: `links_first`: entry k of fine cell (i, j) names coarse column x * 16 + y with x within one of i // 2 and y within one of j // 2, both periodic on the coarse grid. `links_second`: entry k of cell (i, j) names coarse column x * 8 + y with x within one of i // 2 and y within one of j // 2, both periodic on the coarse grid. `links_third`: entry k of cell (i, j) names coarse column x * 4 + y with x within one of i // 2 and y within one of j // 2, both periodic on the coarse grid.
All inputs are finite; a program needn't handle non-finite values.
Results may differ from a plain program's by a relative error of at most 0.0005.
Values may be sent and summed in bfloat16 or wider, within the bound.
A program may use at most 256 MiB of HBM per device.

v0:
```python
from functools import partial
import jax
import jax.numpy as jnp
from jax import lax
from jax.sharding import PartitionSpec as P

DEGREE = 3
upper_edge = 14.0
lower_edge = upper_edge / 8.0


def padded(x, sides, width):
    for axis, dim in sides:
        peers, length = (lax.axis_size(axis), x.shape[dim])
        up = [(i, (i + 1) % peers) for i in range(peers)]
        down = [(j, i) for i, j in up]
        last = lax.slice_in_dim(x, length - width, length, axis=dim)
        initial = lax.slice_in_dim(x, 0, width, axis=dim)
        before = lax.ppermute(last, axis, up)
        after = lax.ppermute(initial, axis, down)
        x = jnp.concatenate([before, x, after], axis=dim)
    return x


def chebyshev(source, initial, operator):
    centre = (upper_edge + lower_edge) / 2.0
    half_width = (upper_edge - lower_edge) / 2.0
    ratio_edge = centre / half_width
    factor = 1.0 / ratio_edge
    residual = source - operator(initial)
    direction = residual / centre
    result = initial
    for sweep_index in range(DEGREE):
        result = result + direction
        if sweep_index + 1 < DEGREE:
            residual = residual - operator(direction)
            factor_next = 1.0 / (2.0 * ratio_edge - factor)
            direction = factor_next * factor * direction + 2.0 * factor_next / half_width * residual
            factor = factor_next
    return result


def line_sum(vector):
    return jnp.roll(vector, 1, 3) + jnp.roll(vector, -1, 3)


def spread_apply(vector, diagonal):
    extended = padded(vector, (("gz", 0), ("gy", 1)), 1)
    beside = extended[2:, 1:-1] + extended[:-2, 1:-1] + extended[1:-1, 2:] + extended[1:-1, :-2]
    beside = beside + line_sum(vector)
    return (6.0 + diagonal[:, :, None, :]) * vector - beside


def slab_apply(vector, diagonal):
    extended = padded(vector, (("gz", 0),), 1)
    beside = extended[2:] + extended[:-2] + jnp.roll(vector, 1, 1) + jnp.roll(vector, -1, 1)
    beside = beside + line_sum(vector)
    return (6.0 + diagonal[:, :, None, :]) * vector - beside


def pack_level(source, initial, diagonal):
    return jnp.concatenate([source, initial, diagonal[:, :, None, :]], axis=2)


def level_smooth(source, initial, diagonal):
    return chebyshev(source, initial, partial(spread_apply, diagonal=diagonal))


def gathered_smooth(source, initial, diagonal):
    copies = source.shape[2]
    gathered = lax.all_gather(pack_level(source, initial, diagonal), "gy", axis=1, tiled=True)
    return chebyshev(
        gathered[:, :, :copies],
        gathered[:, :, copies : 2 * copies],
        partial(slab_apply, diagonal=gathered[:, :, 2 * copies]),
    )


def own_rows(gathered):
    row_count = gathered.shape[1] // lax.axis_size("gy")
    return lax.dynamic_slice_in_dim(gathered, lax.axis_index("gy") * row_count, row_count, 1)


def prolong_local(extended, link_ids, blocks, anchor_row, anchor_col, full_rows, full_cols):
    coarse_row = link_ids // full_cols
    coarse_col = link_ids % full_cols
    local_row = (coarse_row - anchor_row + 1) % full_rows
    local_col = (coarse_col - anchor_col + 1) % full_cols
    flat_index = local_row * extended.shape[1] + local_col
    picked_lines = extended.reshape((-1,) + extended.shape[2:])[flat_index]
    return jnp.einsum("abkrj,abkij->abri", picked_lines, blocks, preferred_element_type=jnp.float32)


def spread_prolong(coarse, link_ids, blocks):
    narrow = coarse.astype(jnp.bfloat16)
    extended = padded(narrow, (("gz", 0), ("gy", 1)), 1)
    return prolong_local(
        extended,
        link_ids,
        blocks,
        lax.axis_index("gz") * coarse.shape[0],
        lax.axis_index("gy") * coarse.shape[1],
        coarse.shape[0] * lax.axis_size("gz"),
        coarse.shape[1] * lax.axis_size("gy"),
    )


def slab_prolong(gathered, link_ids, blocks):
    narrow = gathered.astype(jnp.bfloat16)
    extended = padded(narrow, (("gz", 0),), 1)
    extended = jnp.concatenate([extended[:, -1:], extended, extended[:, :1]], axis=1)
    return prolong_local(
        extended,
        link_ids,
        blocks,
        lax.axis_index("gz") * gathered.shape[0],
        0,
        gathered.shape[0] * lax.axis_size("gz"),
        gathered.shape[1],
    )


def shards(
    source_first,
    source_second,
    source_third,
    source_fourth,
    guess_first,
    guess_second,
    guess_third,
    guess_fourth,
    shift_first,
    shift_second,
    shift_third,
    shift_fourth,
    blocks_first,
    blocks_second,
    blocks_third,
    links_first,
    links_second,
    links_third,
):
    fourth_whole = gathered_smooth(source_fourth, guess_fourth, shift_fourth)
    smooth_fourth = own_rows(fourth_whole)
    start_third = guess_third + slab_prolong(fourth_whole, links_third, blocks_third)
    third_whole = gathered_smooth(source_third, start_third, shift_third)
    smooth_third = own_rows(third_whole)
    start_second = guess_second + slab_prolong(third_whole, links_second, blocks_second)
    smooth_second = level_smooth(source_second, start_second, shift_second)
    start_first = guess_first + spread_prolong(smooth_second, links_first, blocks_first)
    smooth_first = level_smooth(source_first, start_first, shift_first)
    return (smooth_first, smooth_second, smooth_third, smooth_fourth)


def solution(mesh):
    in_specs = (
        P("gz", "gy", None, None),
        P("gz", "gy", None, None),
        P("gz", "gy", None, None),
        P("gz", "gy", None, None),
        P("gz", "gy", None, None),
        P("gz", "gy", None, None),
        P("gz", "gy", None, None),
        P("gz", "gy", None, None),
        P("gz", "gy", None),
        P("gz", "gy", None),
        P("gz", "gy", None),
        P("gz", "gy", None),
        P("gz", "gy", None, None, None),
        P("gz", "gy", None, None, None),
        P("gz", "gy", None, None, None),
        P("gz", "gy", None),
        P("gz", "gy", None),
        P("gz", "gy", None),
    )
    out_specs = (
        P("gz", "gy", None, None),
        P("gz", "gy", None, None),
        P("gz", "gy", None, None),
        P("gz", "gy", None, None),
    )
    return jax.shard_map(shards, mesh=mesh, in_specs=in_specs, out_specs=out_specs, check_vma=False)
```

profile of v0, /device:TPU:0, one launch (start us, length us, event | category | flops | bytes accessed | tf_op | source)
XLA Modules:
  0.0 166.0 jit_solution(16387655743293812934)
XLA Ops:
  0.6 0.8 pad_maximum_fusion.85
  1.5 6.2 %all_gather.6 = f32[1,4,33,128]{3,0,2,1:T(1,128)S(1)} all-gather(f32[1,1,33,128]{3,0,2,1:T(1,128)S(1)} %pad_maximum_fusion.85), channel_id=1, replica_groups=mesh['gz'=8,'gy'=4] {'gy'}, dimensions={1}, use_global_device_ids=true | all-gather | bytes 84480 | tf_op jit(solution)/shard_map/all_gather | solution.py:71
  7.7 2.0 %collective-permute-start.1 = (f32[1,4,16,128]{3,2,1,0:T(8,128)S(1)}, f32[1,4,16,128]{3,2,1,0:T(8,128)S(1)}, u32[]{:S(2)}, u32[]{:S(2)}) collective-permute-start(f32[1,4,16,128]{3,2,1,0:T(8,128)S(1)} %bitcast.49), channel_id=1, source_target_pairs={{0,4},{4,8},{8,12},{12,16},{16,20},{20,24},{24,28},{28,0},{1,5},{5... | collective-permute-start | bytes 98312 | tf_op jit(solution)/shard_map/ppermute | solution.py:19
  9.7 3.1 %collective-permute-start = (f32[1,4,16,128]{3,2,1,0:T(8,128)S(1)}, f32[1,4,16,128]{3,2,1,0:T(8,128)S(1)}, u32[]{:S(2)}, u32[]{:S(2)}) collective-permute-start(f32[1,4,16,128]{3,2,1,0:T(8,128)S(1)} %bitcast.50), channel_id=1, source_target_pairs={{4,0},{8,4},{12,8},{16,12},{20,16},{24,20},{28,24},{0,28},{5,1},{9... | collective-permute-start | bytes 98312 | tf_op jit(solution)/shard_map/ppermute | solution.py:20
  13.1 0.7 compare_select_fusion.10
  13.9 0.7 broadcast_multiply_fusion.5
  14.6 0.8 broadcast_multiply_fusion.3
  15.4 0.7 compare_select_fusion.5
  16.1 0.8 compare_select_fusion
  17.3 4.7 %collective-permute-start.2 = (f32[1,4,16,128]{3,2,1,0:T(8,128)S(1)}, f32[1,4,16,128]{3,2,1,0:T(8,128)S(1)}, u32[]{:S(2)}, u32[]{:S(2)}) collective-permute-start(f32[1,4,16,128]{3,2,1,0:T(8,128)S(1)} %get-tuple-element.28), channel_id=1, source_target_pairs={{4,0},{8,4},{12,8},{16,12},{20,16},{24,20},{28,24},{0,28},{5,1},{9... | collective-permute-start | bytes 98312 | tf_op jit(solution)/shard_map/ppermute | solution.py:20
  22.1 1.7 %collective-permute-done.3 = f32[1,4,16,128]{3,2,1,0:T(8,128)S(1)} collective-permute-done((f32[1,4,16,128]{3,2,1,0:T(8,128)S(1)}, f32[1,4,16,128]{3,2,1,0:T(8,128)S(1)}, u32[]{:S(2)}, u32[]{:S(2)}) %collective-permute-start.3) | collective-permute-done | bytes 32800 | tf_op jit(solution)/shard_map/ppermute | solution.py:19
  24.0 4.8 %collective-permute-start.4 = (f32[1,4,16,128]{3,2,1,0:T(8,128)S(1)}, f32[1,4,16,128]{3,2,1,0:T(8,128)S(1)}, u32[]{:S(2)}, u32[]{:S(2)}) collective-permute-start(f32[1,4,16,128]{3,2,1,0:T(8,128)S(1)} %get-tuple-element.26), channel_id=1, source_target_pairs={{4,0},{8,4},{12,8},{16,12},{20,16},{24,20},{28,24},{0,28},{5,1},{9... | collective-permute-start | bytes 98312 | tf_op jit(solution)/shard_map/ppermute | solution.py:20
  29.0 1.7 %collective-permute-done.5 = f32[1,4,16,128]{3,2,1,0:T(8,128)S(1)} collective-permute-done((f32[1,4,16,128]{3,2,1,0:T(8,128)S(1)}, f32[1,4,16,128]{3,2,1,0:T(8,128)S(1)}, u32[]{:S(2)}, u32[]{:S(2)}) %collective-permute-start.5) | collective-permute-done | bytes 32800 | tf_op jit(solution)/shard_map/ppermute | solution.py:19
  30.8 4.8 %collective-permute-start.7 = (bf16[1,4,16,128]{3,2,1,0:T(8,128)(2,1)S(1)}, bf16[1,4,16,128]{3,2,1,0:T(8,128)(2,1)S(1)}, u32[]{:S(2)}, u32[]{:S(2)}) collective-permute-start(bf16[1,4,16,128]{3,2,1,0:T(8,128)(2,1)S(1)} %get-tuple-element.24), channel_id=1, source_target_pairs={{4,0},{8,4},{12,8},{16,12},{20,16},{24,20},{28,24},{0,28},{5,1},{9... | collective-permute-start | bytes 49160 | tf_op jit(solution)/shard_map/ppermute | solution.py:20
  35.9 1.2 collective-permute-done.7
  37.0 5.0 %collective-permute-done.6 = bf16[1,4,16,128]{3,2,1,0:T(8,128)(2,1)S(1)} collective-permute-done((bf16[1,4,16,128]{3,2,1,0:T(8,128)(2,1)S(1)}, bf16[1,4,16,128]{3,2,1,0:T(8,128)(2,1)S(1)}, u32[]{:S(2)}, u32[]{:S(2)}) %collective-permute-start.6) | collective-permute-done | bytes 16416 | tf_op jit(solution)/shard_map/ppermute | solution.py:19
  42.6 1.1 fusion.2
  43.7 0.8 pad_maximum_fusion.68
  44.5 6.3 %all_gather.7 = f32[2,8,33,128]{3,2,1,0:T(8,128)S(1)} all-gather(f32[2,2,33,128]{3,2,1,0:T(8,128)S(1)} %pad_maximum_fusion.68), channel_id=1, replica_groups=mesh['gz'=8,'gy'=4] {'gy'}, dimensions={1}, use_global_device_ids=true | all-gather | bytes 337920 | tf_op jit(solution)/shard_map/all_gather | solution.py:71
  51.1 2.0 %collective-permute-start.9 = (f32[1,8,16,128]{3,2,1,0:T(8,128)S(1)}, f32[1,8,16,128]{3,2,1,0:T(8,128)S(1)}, u32[]{:S(2)}, u32[]{:S(2)}) collective-permute-start(f32[1,8,16,128]{3,2,1,0:T(8,128)S(1)} %get-tuple-element.55), channel_id=1, source_target_pairs={{0,4},{4,8},{8,12},{12,16},{16,20},{20,24},{24,28},{28,0},{1,5},{5... | collective-permute-start | bytes 196616 | tf_op jit(solution)/shard_map/ppermute | solution.py:19
  53.1 2.3 %collective-permute-done.8 = f32[1,8,16,128]{3,2,1,0:T(8,128)S(1)} collective-permute-done((f32[1,8,16,128]{3,2,1,0:T(8,128)S(1)}, f32[1,8,16,128]{3,2,1,0:T(8,128)S(1)}, u32[]{:S(2)}, u32[]{:S(2)}) %collective-permute-start.8) | collective-permute-done | bytes 65568 | tf_op jit(solution)/shard_map/ppermute | solution.py:20
  55.4 2.8 %collective-permute-done.9 = f32[1,8,16,128]{3,2,1,0:T(8,128)S(1)} collective-permute-done((f32[1,8,16,128]{3,2,1,0:T(8,128)S(1)}, f32[1,8,16,128]{3,2,1,0:T(8,128)S(1)}, u32[]{:S(2)}, u32[]{:S(2)}) %collective-permute-start.9) | collective-permute-done | bytes 65568 | tf_op jit(solution)/shard_map/ppermute | solution.py:19
  58.9 1.8 %collective-permute-start.11 = (f32[1,8,16,128]{3,2,1,0:T(8,128)S(1)}, f32[1,8,16,128]{3,2,1,0:T(8,128)S(1)}, u32[]{:S(2)}, u32[]{:S(2)}) collective-permute-start(f32[1,8,16,128]{3,2,1,0:T(8,128)S(1)} %get-tuple-element.99), channel_id=1, source_target_pairs={{0,4},{4,8},{8,12},{12,16},{16,20},{20,24},{24,28},{28,0},{1,5},{5... | collective-permute-start | bytes 196616 | tf_op jit(solution)/shard_map/ppermute | solution.py:19
  60.7 2.2 %collective-permute-done.10 = f32[1,8,16,128]{3,2,1,0:T(8,128)S(1)} collective-permute-done((f32[1,8,16,128]{3,2,1,0:T(8,128)S(1)}, f32[1,8,16,128]{3,2,1,0:T(8,128)S(1)}, u32[]{:S(2)}, u32[]{:S(2)}) %collective-permute-start.10) | collective-permute-done | bytes 65568 | tf_op jit(solution)/shard_map/ppermute | solution.py:20
  62.9 2.9 %collective-permute-done.11 = f32[1,8,16,128]{3,2,1,0:T(8,128)S(1)} collective-permute-done((f32[1,8,16,128]{3,2,1,0:T(8,128)S(1)}, f32[1,8,16,128]{3,2,1,0:T(8,128)S(1)}, u32[]{:S(2)}, u32[]{:S(2)}) %collective-permute-start.11) | collective-permute-done | bytes 65568 | tf_op jit(solution)/shard_map/ppermute | solution.py:19
  66.3 2.0 %collective-permute-start.13 = (f32[1,8,16,128]{3,2,1,0:T(8,128)S(1)}, f32[1,8,16,128]{3,2,1,0:T(8,128)S(1)}, u32[]{:S(2)}, u32[]{:S(2)}) collective-permute-start(f32[1,8,16,128]{3,2,1,0:T(8,128)S(1)} %get-tuple-element.89), channel_id=1, source_target_pairs={{0,4},{4,8},{8,12},{12,16},{16,20},{20,24},{24,28},{28,0},{1,5},{5... | collective-permute-start | bytes 196616 | tf_op jit(solution)/shard_map/ppermute | solution.py:19
  68.3 2.9 %collective-permute-done.12 = f32[1,8,16,128]{3,2,1,0:T(8,128)S(1)} collective-permute-done((f32[1,8,16,128]{3,2,1,0:T(8,128)S(1)}, f32[1,8,16,128]{3,2,1,0:T(8,128)S(1)}, u32[]{:S(2)}, u32[]{:S(2)}) %collective-permute-start.12) | collective-permute-done | bytes 65568 | tf_op jit(solution)/shard_map/ppermute | solution.py:20
  71.3 2.1 %collective-permute-done.13 = f32[1,8,16,128]{3,2,1,0:T(8,128)S(1)} collective-permute-done((f32[1,8,16,128]{3,2,1,0:T(8,128)S(1)}, f32[1,8,16,128]{3,2,1,0:T(8,128)S(1)}, u32[]{:S(2)}, u32[]{:S(2)}) %collective-permute-start.13) | collective-permute-done | bytes 65568 | tf_op jit(solution)/shard_map/ppermute | solution.py:19
  73.6 4.7 %collective-permute-start.15 = (bf16[1,8,16,128]{3,2,1,0:T(8,128)(2,1)S(1)}, bf16[1,8,16,128]{3,2,1,0:T(8,128)(2,1)S(1)}, u32[]{:S(2)}, u32[]{:S(2)}) collective-permute-start(bf16[1,8,16,128]{3,2,1,0:T(8,128)(2,1)S(1)} %get-tuple-element.123), channel_id=1, source_target_pairs={{4,0},{8,4},{12,8},{16,12},{20,16},{24,20},{28,24},{0,28},{5,1},{9... | collective-permute-start | bytes 98312 | tf_op jit(solution)/shard_map/ppermute | solution.py:20
  78.3 1.9 %collective-permute-done.14 = bf16[1,8,16,128]{3,2,1,0:T(8,128)(2,1)S(1)} collective-permute-done((bf16[1,8,16,128]{3,2,1,0:T(8,128)(2,1)S(1)}, bf16[1,8,16,128]{3,2,1,0:T(8,128)(2,1)S(1)}, u32[]{:S(2)}, u32[]{:S(2)}) %collective-permute-start.14) | collective-permute-done | bytes 32800 | tf_op jit(solution)/shard_map/ppermute | solution.py:19
  81.3 4.9 %collective-permute-start.16 = (f32[1,4,16,128]{3,2,1,0:T(8,128)S(1)}, f32[1,4,16,128]{3,2,1,0:T(8,128)S(1)}, u32[]{:S(2)}, u32[]{:S(2)}) collective-permute-start(f32[1,4,16,128]{3,2,1,0:T(8,128)S(1)} %get-tuple-element.83), channel_id=1, source_target_pairs={{4,0},{8,4},{12,8},{16,12},{20,16},{24,20},{28,24},{0,28},{5,1},{9... | collective-permute-start | bytes 98312 | tf_op jit(solution)/shard_map/ppermute | solution.py:20
  86.2 1.7 %collective-permute-done.17 = f32[1,4,16,128]{3,2,1,0:T(8,128)S(1)} collective-permute-done((f32[1,4,16,128]{3,2,1,0:T(8,128)S(1)}, f32[1,4,16,128]{3,2,1,0:T(8,128)S(1)}, u32[]{:S(2)}, u32[]{:S(2)}) %collective-permute-start.17) | collective-permute-done | bytes 32800 | tf_op jit(solution)/shard_map/ppermute | solution.py:19
  88.6 1.1 collective-permute-done.18
  89.8 2.2 %collective-permute-done.19 = f32[6,1,16,128]{3,2,1,0:T(8,128)S(1)} collective-permute-done((f32[6,1,16,128]{3,2,1,0:T(8,128)S(1)}, f32[6,1,16,128]{3,2,1,0:T(8,128)S(1)}, u32[]{:S(2)}, u32[]{:S(2)}) %collective-permute-start.19) | collective-permute-done | bytes 49184 | tf_op jit(solution)/shard_map/ppermute | solution.py:19
  92.2 4.8 %collective-permute-start.20 = (f32[1,4,16,128]{3,2,1,0:T(8,128)S(1)}, f32[1,4,16,128]{3,2,1,0:T(8,128)S(1)}, u32[]{:S(2)}, u32[]{:S(2)}) collective-permute-start(f32[1,4,16,128]{3,2,1,0:T(8,128)S(1)} %get-tuple-element.77), channel_id=1, source_target_pairs={{4,0},{8,4},{12,8},{16,12},{20,16},{24,20},{28,24},{0,28},{5,1},{9... | collective-permute-start | bytes 98312 | tf_op jit(solution)/shard_map/ppermute | solution.py:20
  97.2 1.7 %collective-permute-done.21 = f32[1,4,16,128]{3,2,1,0:T(8,128)S(1)} collective-permute-done((f32[1,4,16,128]{3,2,1,0:T(8,128)S(1)}, f32[1,4,16,128]{3,2,1,0:T(8,128)S(1)}, u32[]{:S(2)}, u32[]{:S(2)}) %collective-permute-start.21) | collective-permute-done | bytes 32800 | tf_op jit(solution)/shard_map/ppermute | solution.py:19
  99.6 1.1 collective-permute-done.22
  100.7 1.8 %collective-permute-done.23 = f32[6,1,16,128]{3,2,1,0:T(8,128)S(1)} collective-permute-done((f32[6,1,16,128]{3,2,1,0:T(8,128)S(1)}, f32[6,1,16,128]{3,2,1,0:T(8,128)S(1)}, u32[]{:S(2)}, u32[]{:S(2)}) %collective-permute-start.23) | collective-permute-done | bytes 49184 | tf_op jit(solution)/shard_map/ppermute | solution.py:19
  102.8 4.8 %collective-permute-start.24 = (f32[1,4,16,128]{3,2,1,0:T(8,128)S(1)}, f32[1,4,16,128]{3,2,1,0:T(8,128)S(1)}, u32[]{:S(2)}, u32[]{:S(2)}) collective-permute-start(f32[1,4,16,128]{3,2,1,0:T(8,128)S(1)} %get-tuple-element.71), channel_id=1, source_target_pairs={{4,0},{8,4},{12,8},{16,12},{20,16},{24,20},{28,24},{0,28},{5,1},{9... | collective-permute-start | bytes 98312 | tf_op jit(solution)/shard_map/ppermute | solution.py:20
  107.7 1.7 %collective-permute-done.25 = f32[1,4,16,128]{3,2,1,0:T(8,128)S(1)} collective-permute-done((f32[1,4,16,128]{3,2,1,0:T(8,128)S(1)}, f32[1,4,16,128]{3,2,1,0:T(8,128)S(1)}, u32[]{:S(2)}, u32[]{:S(2)}) %collective-permute-start.25) | collective-permute-done | bytes 32800 | tf_op jit(solution)/shard_map/ppermute | solution.py:19
  110.1 1.1 collective-permute-done.26
  111.3 1.9 %collective-permute-done.27 = f32[6,1,16,128]{3,2,1,0:T(8,128)S(1)} collective-permute-done((f32[6,1,16,128]{3,2,1,0:T(8,128)S(1)}, f32[6,1,16,128]{3,2,1,0:T(8,128)S(1)}, u32[]{:S(2)}, u32[]{:S(2)}) %collective-permute-start.27) | collective-permute-done | bytes 49184 | tf_op jit(solution)/shard_map/ppermute | solution.py:19
  113.1 0.8 fusion.102
  114.0 4.8 %collective-permute-start.29 = (bf16[1,4,16,128]{3,2,1,0:T(8,128)(2,1)S(1)}, bf16[1,4,16,128]{3,2,1,0:T(8,128)(2,1)S(1)}, u32[]{:S(2)}, u32[]{:S(2)}) collective-permute-start(bf16[1,4,16,128]{3,2,1,0:T(8,128)(2,1)S(1)} %get-tuple-element.121), channel_id=1, source_target_pairs={{4,0},{8,4},{12,8},{16,12},{20,16},{24,20},{28,24},{0,28},{5,1},{9... | collective-permute-start | bytes 49160 | tf_op jit(solution)/shard_map/ppermute | solution.py:20
  119.3 1.1 collective-permute-done.28
  120.5 1.7 %collective-permute-start.31 = (bf16[6,1,16,128]{3,2,1,0:T(8,128)(2,1)S(1)}, bf16[6,1,16,128]{3,2,1,0:T(8,128)(2,1)S(1)}, u32[]{:S(2)}, u32[]{:S(2)}) collective-permute-start(bf16[6,1,16,128]{3,2,1,0:T(8,128)(2,1)S(1)} %get-tuple-element.109), channel_id=1, source_target_pairs={{1,0},{2,1},{3,2},{0,3},{5,4},{6,5},{7,6},{4,7},{9,8},{10,9},{11,1... | collective-permute-start | bytes 73736 | tf_op jit(solution)/shard_map/ppermute | solution.py:20
  122.3 0.6 constant_dynamic-slice_fusion.1
  122.9 0.9 collective-permute-done.30
  123.8 0.7 gather_fusion.2
  124.5 3.4 %fusion = f32[8,8,16,128]{3,2,1,0:T(8,128)S(1)} fusion(f32[8,8,16,128]{3,2,1,0:T(8,128)S(1)} %copy-done.2, bf16[8,8,2,16,128]{4,3,2,1,0:T(8,128)(2,1)S(1)} %bitcast.46, bf16[8,8,2,128,128]{4,3,2,1,0:T(8,128)(2,1)} %param.30), kind=kOutput, calls=%fused_computation.4 | convolution fusion | flops 67239936 | bytes 5767168 | tf_op jit(solution)/shard_map/abkrj,abkij->abri/dot_general | solution.py:91
  128.1 4.8 %collective-permute-start.32 = (f32[1,8,16,128]{3,2,1,0:T(8,128)S(1)}, f32[1,8,16,128]{3,2,1,0:T(8,128)S(1)}, u32[]{:S(2)}, u32[]{:S(2)}) collective-permute-start(f32[1,8,16,128]{3,2,1,0:T(8,128)S(1)} %get-tuple-element.49), channel_id=1, source_target_pairs={{4,0},{8,4},{12,8},{16,12},{20,16},{24,20},{28,24},{0,28},{5,1},{9... | collective-permute-start | bytes 196616 | tf_op jit(solution)/shard_map/ppermute | solution.py:20
  133.0 2.3 %collective-permute-done.33 = f32[1,8,16,128]{3,2,1,0:T(8,128)S(1)} collective-permute-done((f32[1,8,16,128]{3,2,1,0:T(8,128)S(1)}, f32[1,8,16,128]{3,2,1,0:T(8,128)S(1)}, u32[]{:S(2)}, u32[]{:S(2)}) %collective-permute-start.33) | collective-permute-done | bytes 65568 | tf_op jit(solution)/shard_map/ppermute | solution.py:19
  135.3 0.9 collective-permute-start.34
  136.4 2.2 %collective-permute-done.34 = f32[10,1,16,128]{3,2,1,0:T(8,128)S(1)} collective-permute-done((f32[10,1,16,128]{3,2,1,0:T(8,128)S(1)}, f32[10,1,16,128]{3,2,1,0:T(8,128)S(1)}, u32[]{:S(2)}, u32[]{:S(2)}) %collective-permute-start.34) | collective-permute-done | bytes 81952 | tf_op jit(solution)/shard_map/ppermute | solution.py:20
  138.6 2.0 %collective-permute-done.35 = f32[10,1,16,128]{3,2,1,0:T(8,128)S(1)} collective-permute-done((f32[10,1,16,128]{3,2,1,0:T(8,128)S(1)}, f32[10,1,16,128]{3,2,1,0:T(8,128)S(1)}, u32[]{:S(2)}, u32[]{:S(2)}) %collective-permute-start.35) | collective-permute-done | bytes 81952 | tf_op jit(solution)/shard_map/ppermute | solution.py:19
  141.1 5.0 %collective-permute-start.36 = (f32[1,8,16,128]{3,2,1,0:T(8,128)S(1)}, f32[1,8,16,128]{3,2,1,0:T(8,128)S(1)}, u32[]{:S(2)}, u32[]{:S(2)}) collective-permute-start(f32[1,8,16,128]{3,2,1,0:T(8,128)S(1)} %get-tuple-element.43), channel_id=1, source_target_pairs={{4,0},{8,4},{12,8},{16,12},{20,16},{24,20},{28,24},{0,28},{5,1},{9... | collective-permute-start | bytes 196616 | tf_op jit(solution)/shard_map/ppermute | solution.py:20
  146.3 2.0 %collective-permute-done.37 = f32[1,8,16,128]{3,2,1,0:T(8,128)S(1)} collective-permute-done((f32[1,8,16,128]{3,2,1,0:T(8,128)S(1)}, f32[1,8,16,128]{3,2,1,0:T(8,128)S(1)}, u32[]{:S(2)}, u32[]{:S(2)}) %collective-permute-start.37) | collective-permute-done | bytes 65568 | tf_op jit(solution)/shard_map/ppermute | solution.py:19
  149.1 1.7 %collective-permute-done.38 = f32[10,1,16,128]{3,2,1,0:T(8,128)S(1)} collective-permute-done((f32[10,1,16,128]{3,2,1,0:T(8,128)S(1)}, f32[10,1,16,128]{3,2,1,0:T(8,128)S(1)}, u32[]{:S(2)}, u32[]{:S(2)}) %collective-permute-start.38) | collective-permute-done | bytes 81952 | tf_op jit(solution)/shard_map/ppermute | solution.py:20
  150.8 1.8 %collective-permute-done.39 = f32[10,1,16,128]{3,2,1,0:T(8,128)S(1)} collective-permute-done((f32[10,1,16,128]{3,2,1,0:T(8,128)S(1)}, f32[10,1,16,128]{3,2,1,0:T(8,128)S(1)}, u32[]{:S(2)}, u32[]{:S(2)}) %collective-permute-start.39) | collective-permute-done | bytes 81952 | tf_op jit(solution)/shard_map/ppermute | solution.py:19
  153.2 4.8 %collective-permute-start.40 = (f32[1,8,16,128]{3,2,1,0:T(8,128)S(1)}, f32[1,8,16,128]{3,2,1,0:T(8,128)S(1)}, u32[]{:S(2)}, u32[]{:S(2)}) collective-permute-start(f32[1,8,16,128]{3,2,1,0:T(8,128)S(1)} %get-tuple-element.41), channel_id=1, source_target_pairs={{4,0},{8,4},{12,8},{16,12},{20,16},{24,20},{28,24},{0,28},{5,1},{9... | collective-permute-start | bytes 196616 | tf_op jit(solution)/shard_map/ppermute | solution.py:20
  158.2 2.0 %collective-permute-done.41 = f32[1,8,16,128]{3,2,1,0:T(8,128)S(1)} collective-permute-done((f32[1,8,16,128]{3,2,1,0:T(8,128)S(1)}, f32[1,8,16,128]{3,2,1,0:T(8,128)S(1)}, u32[]{:S(2)}, u32[]{:S(2)}) %collective-permute-start.41) | collective-permute-done | bytes 65568 | tf_op jit(solution)/shard_map/ppermute | solution.py:19
  161.0 1.5 collective-permute-done.42
  162.5 2.1 %collective-permute-done.43 = f32[10,1,16,128]{3,2,1,0:T(8,128)S(1)} collective-permute-done((f32[10,1,16,128]{3,2,1,0:T(8,128)S(1)}, f32[10,1,16,128]{3,2,1,0:T(8,128)S(1)}, u32[]{:S(2)}, u32[]{:S(2)}) %collective-permute-start.43) | collective-permute-done | bytes 81952 | tf_op jit(solution)/shard_map/ppermute | solution.py:19
  164.7 1.3 fusion.9
  (134 shorter events, 11.8 us)
Async XLA Ops:
  0.6 80.2 %copy-start = (bf16[4,4,2,128,128]{4,3,2,1,0:T(8,128)(2,1)S(1)}, bf16[4,4,2,128,128]{4,3,2,1,0:T(8,128)(2,1)}, u32[]{:S(2)}) copy-start(bf16[4,4,2,128,128]{4,3,2,1,0:T(8,128)(2,1)} %param.31) | copy-start | bytes 3145732
  7.7 9.4 %collective-permute-start.1 = (f32[1,4,16,128]{3,2,1,0:T(8,128)S(1)}, f32[1,4,16,128]{3,2,1,0:T(8,128)S(1)}, u32[]{:S(2)}, u32[]{:S(2)}) collective-permute-start(f32[1,4,16,128]{3,2,1,0:T(8,128)S(1)} %bitcast.49), channel_id=1, source_target_pairs={{0,4},{4,8},{8,12},{12,16},{16,20},{20,24},{24,28},{28,0},{1,5},{5... | collective-permute-start | bytes 98312 | tf_op jit(solution)/shard_map/ppermute | solution.py:19
  9.7 7.4 %collective-permute-start = (f32[1,4,16,128]{3,2,1,0:T(8,128)S(1)}, f32[1,4,16,128]{3,2,1,0:T(8,128)S(1)}, u32[]{:S(2)}, u32[]{:S(2)}) collective-permute-start(f32[1,4,16,128]{3,2,1,0:T(8,128)S(1)} %bitcast.50), channel_id=1, source_target_pairs={{4,0},{8,4},{12,8},{16,12},{20,16},{24,20},{28,24},{0,28},{5,1},{9... | collective-permute-start | bytes 98312 | tf_op jit(solution)/shard_map/ppermute | solution.py:20
  17.2 6.7 %collective-permute-start.3 = (f32[1,4,16,128]{3,2,1,0:T(8,128)S(1)}, f32[1,4,16,128]{3,2,1,0:T(8,128)S(1)}, u32[]{:S(2)}, u32[]{:S(2)}) collective-permute-start(f32[1,4,16,128]{3,2,1,0:T(8,128)S(1)} %get-tuple-element.28), channel_id=1, source_target_pairs={{0,4},{4,8},{8,12},{12,16},{16,20},{20,24},{24,28},{28,0},{1,5},{5... | collective-permute-start | bytes 98312 | tf_op jit(solution)/shard_map/ppermute | solution.py:19
  17.3 6.6 %collective-permute-start.2 = (f32[1,4,16,128]{3,2,1,0:T(8,128)S(1)}, f32[1,4,16,128]{3,2,1,0:T(8,128)S(1)}, u32[]{:S(2)}, u32[]{:S(2)}) collective-permute-start(f32[1,4,16,128]{3,2,1,0:T(8,128)S(1)} %get-tuple-element.28), channel_id=1, source_target_pairs={{4,0},{8,4},{12,8},{16,12},{20,16},{24,20},{28,24},{0,28},{5,1},{9... | collective-permute-start | bytes 98312 | tf_op jit(solution)/shard_map/ppermute | solution.py:20
  24.0 6.7 %collective-permute-start.5 = (f32[1,4,16,128]{3,2,1,0:T(8,128)S(1)}, f32[1,4,16,128]{3,2,1,0:T(8,128)S(1)}, u32[]{:S(2)}, u32[]{:S(2)}) collective-permute-start(f32[1,4,16,128]{3,2,1,0:T(8,128)S(1)} %get-tuple-element.26), channel_id=1, source_target_pairs={{0,4},{4,8},{8,12},{12,16},{16,20},{20,24},{24,28},{28,0},{1,5},{5... | collective-permute-start | bytes 98312 | tf_op jit(solution)/shard_map/ppermute | solution.py:19
  24.0 6.6 %collective-permute-start.4 = (f32[1,4,16,128]{3,2,1,0:T(8,128)S(1)}, f32[1,4,16,128]{3,2,1,0:T(8,128)S(1)}, u32[]{:S(2)}, u32[]{:S(2)}) collective-permute-start(f32[1,4,16,128]{3,2,1,0:T(8,128)S(1)} %get-tuple-element.26), channel_id=1, source_target_pairs={{4,0},{8,4},{12,8},{16,12},{20,16},{24,20},{28,24},{0,28},{5,1},{9... | collective-permute-start | bytes 98312 | tf_op jit(solution)/shard_map/ppermute | solution.py:20
  30.8 6.3 %collective-permute-start.7 = (bf16[1,4,16,128]{3,2,1,0:T(8,128)(2,1)S(1)}, bf16[1,4,16,128]{3,2,1,0:T(8,128)(2,1)S(1)}, u32[]{:S(2)}, u32[]{:S(2)}) collective-permute-start(bf16[1,4,16,128]{3,2,1,0:T(8,128)(2,1)S(1)} %get-tuple-element.24), channel_id=1, source_target_pairs={{4,0},{8,4},{12,8},{16,12},{20,16},{24,20},{28,24},{0,28},{5,1},{9... | collective-permute-start | bytes 49160 | tf_op jit(solution)/shard_map/ppermute | solution.py:20
  35.6 6.4 %collective-permute-start.6 = (bf16[1,4,16,128]{3,2,1,0:T(8,128)(2,1)S(1)}, bf16[1,4,16,128]{3,2,1,0:T(8,128)(2,1)S(1)}, u32[]{:S(2)}, u32[]{:S(2)}) collective-permute-start(bf16[1,4,16,128]{3,2,1,0:T(8,128)(2,1)S(1)} %get-tuple-element.24), channel_id=1, source_target_pairs={{0,4},{4,8},{8,12},{12,16},{16,20},{20,24},{24,28},{28,0},{1,5},{5... | collective-permute-start | bytes 49160 | tf_op jit(solution)/shard_map/ppermute | solution.py:19
  51.0 4.4 %collective-permute-start.8 = (f32[1,8,16,128]{3,2,1,0:T(8,128)S(1)}, f32[1,8,16,128]{3,2,1,0:T(8,128)S(1)}, u32[]{:S(2)}, u32[]{:S(2)}) collective-permute-start(f32[1,8,16,128]{3,2,1,0:T(8,128)S(1)} %get-tuple-element.54), channel_id=1, source_target_pairs={{4,0},{8,4},{12,8},{16,12},{20,16},{24,20},{28,24},{0,28},{5,1},{9... | collective-permute-start | bytes 196616 | tf_op jit(solution)/shard_map/ppermute | solution.py:20
  51.1 7.1 %collective-permute-start.9 = (f32[1,8,16,128]{3,2,1,0:T(8,128)S(1)}, f32[1,8,16,128]{3,2,1,0:T(8,128)S(1)}, u32[]{:S(2)}, u32[]{:S(2)}) collective-permute-start(f32[1,8,16,128]{3,2,1,0:T(8,128)S(1)} %get-tuple-element.55), channel_id=1, source_target_pairs={{0,4},{4,8},{8,12},{12,16},{16,20},{20,24},{24,28},{28,0},{1,5},{5... | collective-permute-start | bytes 196616 | tf_op jit(solution)/shard_map/ppermute | solution.py:19
  58.2 22.6 %copy-start.4 = (f32[4,4,16,128]{3,2,1,0:T(8,128)S(1)}, f32[4,4,16,128]{3,2,1,0:T(8,128)}, u32[]{:S(2)}) copy-start(f32[4,4,16,128]{3,2,1,0:T(8,128)} %param.23) | copy-start | bytes 393220
  58.6 4.3 %collective-permute-start.10 = (f32[1,8,16,128]{3,2,1,0:T(8,128)S(1)}, f32[1,8,16,128]{3,2,1,0:T(8,128)S(1)}, u32[]{:S(2)}, u32[]{:S(2)}) collective-permute-start(f32[1,8,16,128]{3,2,1,0:T(8,128)S(1)} %get-tuple-element.98), channel_id=1, source_target_pairs={{4,0},{8,4},{12,8},{16,12},{20,16},{24,20},{28,24},{0,28},{5,1},{9... | collective-permute-start | bytes 196616 | tf_op jit(solution)/shard_map/ppermute | solution.py:20
  58.9 7.0 %collective-permute-start.11 = (f32[1,8,16,128]{3,2,1,0:T(8,128)S(1)}, f32[1,8,16,128]{3,2,1,0:T(8,128)S(1)}, u32[]{:S(2)}, u32[]{:S(2)}) collective-permute-start(f32[1,8,16,128]{3,2,1,0:T(8,128)S(1)} %get-tuple-element.99), channel_id=1, source_target_pairs={{0,4},{4,8},{8,12},{12,16},{16,20},{20,24},{24,28},{28,0},{1,5},{5... | collective-permute-start | bytes 196616 | tf_op jit(solution)/shard_map/ppermute | solution.py:19
  65.8 26.2 %copy-start.3 = (f32[4,4,16,128]{3,2,1,0:T(8,128)S(1)}, f32[4,4,16,128]{3,2,1,0:T(8,128)}, u32[]{:S(2)}) copy-start(f32[4,4,16,128]{3,2,1,0:T(8,128)} %param.19) | copy-start | bytes 393220
  66.2 5.0 %collective-permute-start.12 = (f32[1,8,16,128]{3,2,1,0:T(8,128)S(1)}, f32[1,8,16,128]{3,2,1,0:T(8,128)S(1)}, u32[]{:S(2)}, u32[]{:S(2)}) collective-permute-start(f32[1,8,16,128]{3,2,1,0:T(8,128)S(1)} %get-tuple-element.88), channel_id=1, source_target_pairs={{4,0},{8,4},{12,8},{16,12},{20,16},{24,20},{28,24},{0,28},{5,1},{9... | collective-permute-start | bytes 196616 | tf_op jit(solution)/shard_map/ppermute | solution.py:20
  66.3 7.0 %collective-permute-start.13 = (f32[1,8,16,128]{3,2,1,0:T(8,128)S(1)}, f32[1,8,16,128]{3,2,1,0:T(8,128)S(1)}, u32[]{:S(2)}, u32[]{:S(2)}) collective-permute-start(f32[1,8,16,128]{3,2,1,0:T(8,128)S(1)} %get-tuple-element.89), channel_id=1, source_target_pairs={{0,4},{4,8},{8,12},{12,16},{16,20},{20,24},{24,28},{28,0},{1,5},{5... | collective-permute-start | bytes 196616 | tf_op jit(solution)/shard_map/ppermute | solution.py:19
  73.5 6.7 %collective-permute-start.14 = (bf16[1,8,16,128]{3,2,1,0:T(8,128)(2,1)S(1)}, bf16[1,8,16,128]{3,2,1,0:T(8,128)(2,1)S(1)}, u32[]{:S(2)}, u32[]{:S(2)}) collective-permute-start(bf16[1,8,16,128]{3,2,1,0:T(8,128)(2,1)S(1)} %get-tuple-element.122), channel_id=1, source_target_pairs={{0,4},{4,8},{8,12},{12,16},{16,20},{20,24},{24,28},{28,0},{1,5},{5... | collective-permute-start | bytes 98312 | tf_op jit(solution)/shard_map/ppermute | solution.py:19
  73.6 6.6 %collective-permute-start.15 = (bf16[1,8,16,128]{3,2,1,0:T(8,128)(2,1)S(1)}, bf16[1,8,16,128]{3,2,1,0:T(8,128)(2,1)S(1)}, u32[]{:S(2)}, u32[]{:S(2)}) collective-permute-start(bf16[1,8,16,128]{3,2,1,0:T(8,128)(2,1)S(1)} %get-tuple-element.123), channel_id=1, source_target_pairs={{4,0},{8,4},{12,8},{16,12},{20,16},{24,20},{28,24},{0,28},{5,1},{9... | collective-permute-start | bytes 98312 | tf_op jit(solution)/shard_map/ppermute | solution.py:20
  81.2 6.8 %collective-permute-start.17 = (f32[1,4,16,128]{3,2,1,0:T(8,128)S(1)}, f32[1,4,16,128]{3,2,1,0:T(8,128)S(1)}, u32[]{:S(2)}, u32[]{:S(2)}) collective-permute-start(f32[1,4,16,128]{3,2,1,0:T(8,128)S(1)} %get-tuple-element.82), channel_id=1, source_target_pairs={{0,4},{4,8},{8,12},{12,16},{16,20},{20,24},{24,28},{28,0},{1,5},{5... | collective-permute-start | bytes 98312 | tf_op jit(solution)/shard_map/ppermute | solution.py:19
  81.3 6.7 %collective-permute-start.16 = (f32[1,4,16,128]{3,2,1,0:T(8,128)S(1)}, f32[1,4,16,128]{3,2,1,0:T(8,128)S(1)}, u32[]{:S(2)}, u32[]{:S(2)}) collective-permute-start(f32[1,4,16,128]{3,2,1,0:T(8,128)S(1)} %get-tuple-element.83), channel_id=1, source_target_pairs={{4,0},{8,4},{12,8},{16,12},{20,16},{24,20},{28,24},{0,28},{5,1},{9... | collective-permute-start | bytes 98312 | tf_op jit(solution)/shard_map/ppermute | solution.py:20
  88.0 1.8 %collective-permute-start.18 = (f32[6,1,16,128]{3,2,1,0:T(8,128)S(1)}, f32[6,1,16,128]{3,2,1,0:T(8,128)S(1)}, u32[]{:S(2)}, u32[]{:S(2)}) collective-permute-start(f32[6,1,16,128]{3,2,1,0:T(8,128)S(1)} %get-tuple-element.68), channel_id=1, source_target_pairs={{1,0},{2,1},{3,2},{0,3},{5,4},{6,5},{7,6},{4,7},{9,8},{10,9},{11,1... | collective-permute-start | bytes 147464 | tf_op jit(solution)/shard_map/ppermute | solution.py:20
  88.1 3.9 %collective-permute-start.19 = (f32[6,1,16,128]{3,2,1,0:T(8,128)S(1)}, f32[6,1,16,128]{3,2,1,0:T(8,128)S(1)}, u32[]{:S(2)}, u32[]{:S(2)}) collective-permute-start(f32[6,1,16,128]{3,2,1,0:T(8,128)S(1)} %get-tuple-element.69), channel_id=1, source_target_pairs={{0,1},{1,2},{2,3},{3,0},{4,5},{5,6},{6,7},{7,4},{8,9},{9,10},{10,1... | collective-permute-start | bytes 147464 | tf_op jit(solution)/shard_map/ppermute | solution.py:19
  92.0 32.5 %copy-start.2 = (f32[8,8,16,128]{3,2,1,0:T(8,128)S(1)}, f32[8,8,16,128]{3,2,1,0:T(8,128)}, u32[]{:S(2)}) copy-start(f32[8,8,16,128]{3,2,1,0:T(8,128)} %param.22) | copy-start | bytes 1572868
  92.2 6.7 %collective-permute-start.21 = (f32[1,4,16,128]{3,2,1,0:T(8,128)S(1)}, f32[1,4,16,128]{3,2,1,0:T(8,128)S(1)}, u32[]{:S(2)}, u32[]{:S(2)}) collective-permute-start(f32[1,4,16,128]{3,2,1,0:T(8,128)S(1)} %get-tuple-element.76), channel_id=1, source_target_pairs={{0,4},{4,8},{8,12},{12,16},{16,20},{20,24},{24,28},{28,0},{1,5},{5... | collective-permute-start | bytes 98312 | tf_op jit(solution)/shard_map/ppermute | solution.py:19
  92.2 6.7 %collective-permute-start.20 = (f32[1,4,16,128]{3,2,1,0:T(8,128)S(1)}, f32[1,4,16,128]{3,2,1,0:T(8,128)S(1)}, u32[]{:S(2)}, u32[]{:S(2)}) collective-permute-start(f32[1,4,16,128]{3,2,1,0:T(8,128)S(1)} %get-tuple-element.77), channel_id=1, source_target_pairs={{4,0},{8,4},{12,8},{16,12},{20,16},{24,20},{28,24},{0,28},{5,1},{9... | collective-permute-start | bytes 98312 | tf_op jit(solution)/shard_map/ppermute | solution.py:20
  98.9 1.8 %collective-permute-start.22 = (f32[6,1,16,128]{3,2,1,0:T(8,128)S(1)}, f32[6,1,16,128]{3,2,1,0:T(8,128)S(1)}, u32[]{:S(2)}, u32[]{:S(2)}) collective-permute-start(f32[6,1,16,128]{3,2,1,0:T(8,128)S(1)} %get-tuple-element.66), channel_id=1, source_target_pairs={{1,0},{2,1},{3,2},{0,3},{5,4},{6,5},{7,6},{4,7},{9,8},{10,9},{11,1... | collective-permute-start | bytes 147464 | tf_op jit(solution)/shard_map/ppermute | solution.py:20
  99.0 3.6 %collective-permute-start.23 = (f32[6,1,16,128]{3,2,1,0:T(8,128)S(1)}, f32[6,1,16,128]{3,2,1,0:T(8,128)S(1)}, u32[]{:S(2)}, u32[]{:S(2)}) collective-permute-start(f32[6,1,16,128]{3,2,1,0:T(8,128)S(1)} %get-tuple-element.67), channel_id=1, source_target_pairs={{0,1},{1,2},{2,3},{3,0},{4,5},{5,6},{6,7},{7,4},{8,9},{9,10},{10,1... | collective-permute-start | bytes 147464 | tf_op jit(solution)/shard_map/ppermute | solution.py:19
  102.7 6.7 %collective-permute-start.25 = (f32[1,4,16,128]{3,2,1,0:T(8,128)S(1)}, f32[1,4,16,128]{3,2,1,0:T(8,128)S(1)}, u32[]{:S(2)}, u32[]{:S(2)}) collective-permute-start(f32[1,4,16,128]{3,2,1,0:T(8,128)S(1)} %get-tuple-element.70), channel_id=1, source_target_pairs={{0,4},{4,8},{8,12},{12,16},{16,20},{20,24},{24,28},{28,0},{1,5},{5... | collective-permute-start | bytes 98312 | tf_op jit(solution)/shard_map/ppermute | solution.py:19
  102.8 6.7 %collective-permute-start.24 = (f32[1,4,16,128]{3,2,1,0:T(8,128)S(1)}, f32[1,4,16,128]{3,2,1,0:T(8,128)S(1)}, u32[]{:S(2)}, u32[]{:S(2)}) collective-permute-start(f32[1,4,16,128]{3,2,1,0:T(8,128)S(1)} %get-tuple-element.71), channel_id=1, source_target_pairs={{4,0},{8,4},{12,8},{16,12},{20,16},{24,20},{28,24},{0,28},{5,1},{9... | collective-permute-start | bytes 98312 | tf_op jit(solution)/shard_map/ppermute | solution.py:20
  109.4 1.8 %collective-permute-start.26 = (f32[6,1,16,128]{3,2,1,0:T(8,128)S(1)}, f32[6,1,16,128]{3,2,1,0:T(8,128)S(1)}, u32[]{:S(2)}, u32[]{:S(2)}) collective-permute-start(f32[6,1,16,128]{3,2,1,0:T(8,128)S(1)} %get-tuple-element.64), channel_id=1, source_target_pairs={{1,0},{2,1},{3,2},{0,3},{5,4},{6,5},{7,6},{4,7},{9,8},{10,9},{11,1... | collective-permute-start | bytes 147464 | tf_op jit(solution)/shard_map/ppermute | solution.py:20
  109.5 3.6 %collective-permute-start.27 = (f32[6,1,16,128]{3,2,1,0:T(8,128)S(1)}, f32[6,1,16,128]{3,2,1,0:T(8,128)S(1)}, u32[]{:S(2)}, u32[]{:S(2)}) collective-permute-start(f32[6,1,16,128]{3,2,1,0:T(8,128)S(1)} %get-tuple-element.65), channel_id=1, source_target_pairs={{0,1},{1,2},{2,3},{3,0},{4,5},{5,6},{6,7},{7,4},{8,9},{9,10},{10,1... | collective-permute-start | bytes 147464 | tf_op jit(solution)/shard_map/ppermute | solution.py:19
  114.0 6.5 %collective-permute-start.28 = (bf16[1,4,16,128]{3,2,1,0:T(8,128)(2,1)S(1)}, bf16[1,4,16,128]{3,2,1,0:T(8,128)(2,1)S(1)}, u32[]{:S(2)}, u32[]{:S(2)}) collective-permute-start(bf16[1,4,16,128]{3,2,1,0:T(8,128)(2,1)S(1)} %get-tuple-element.120), channel_id=1, source_target_pairs={{0,4},{4,8},{8,12},{12,16},{16,20},{20,24},{24,28},{28,0},{1,5},{5... | collective-permute-start | bytes 49160 | tf_op jit(solution)/shard_map/ppermute | solution.py:19
  114.0 6.5 %collective-permute-start.29 = (bf16[1,4,16,128]{3,2,1,0:T(8,128)(2,1)S(1)}, bf16[1,4,16,128]{3,2,1,0:T(8,128)(2,1)S(1)}, u32[]{:S(2)}, u32[]{:S(2)}) collective-permute-start(bf16[1,4,16,128]{3,2,1,0:T(8,128)(2,1)S(1)} %get-tuple-element.121), channel_id=1, source_target_pairs={{4,0},{8,4},{12,8},{16,12},{20,16},{24,20},{28,24},{0,28},{5,1},{9... | collective-permute-start | bytes 49160 | tf_op jit(solution)/shard_map/ppermute | solution.py:20
  120.5 3.3 %collective-permute-start.30 = (bf16[6,1,16,128]{3,2,1,0:T(8,128)(2,1)S(1)}, bf16[6,1,16,128]{3,2,1,0:T(8,128)(2,1)S(1)}, u32[]{:S(2)}, u32[]{:S(2)}) collective-permute-start(bf16[6,1,16,128]{3,2,1,0:T(8,128)(2,1)S(1)} %get-tuple-element.108), channel_id=1, source_target_pairs={{0,1},{1,2},{2,3},{3,0},{4,5},{5,6},{6,7},{7,4},{8,9},{9,10},{10,1... | collective-permute-start | bytes 73736 | tf_op jit(solution)/shard_map/ppermute | solution.py:19
  120.5 3.3 %collective-permute-start.31 = (bf16[6,1,16,128]{3,2,1,0:T(8,128)(2,1)S(1)}, bf16[6,1,16,128]{3,2,1,0:T(8,128)(2,1)S(1)}, u32[]{:S(2)}, u32[]{:S(2)}) collective-permute-start(bf16[6,1,16,128]{3,2,1,0:T(8,128)(2,1)S(1)} %get-tuple-element.109), channel_id=1, source_target_pairs={{1,0},{2,1},{3,2},{0,3},{5,4},{6,5},{7,6},{4,7},{9,8},{10,9},{11,1... | collective-permute-start | bytes 73736 | tf_op jit(solution)/shard_map/ppermute | solution.py:20
  124.5 16.0 %copy-start.1 = (f32[8,8,16,128]{3,2,1,0:T(8,128)S(1)}, f32[8,8,16,128]{3,2,1,0:T(8,128)}, u32[]{:S(2)}) copy-start(f32[8,8,16,128]{3,2,1,0:T(8,128)} %param.18) | copy-start | bytes 1572868
  128.0 7.3 %collective-permute-start.33 = (f32[1,8,16,128]{3,2,1,0:T(8,128)S(1)}, f32[1,8,16,128]{3,2,1,0:T(8,128)S(1)}, u32[]{:S(2)}, u32[]{:S(2)}) collective-permute-start(f32[1,8,16,128]{3,2,1,0:T(8,128)S(1)} %get-tuple-element.48), channel_id=1, source_target_pairs={{0,4},{4,8},{8,12},{12,16},{16,20},{20,24},{24,28},{28,0},{1,5},{5... | collective-permute-start | bytes 196616 | tf_op jit(solution)/shard_map/ppermute | solution.py:19
  128.1 7.3 %collective-permute-start.32 = (f32[1,8,16,128]{3,2,1,0:T(8,128)S(1)}, f32[1,8,16,128]{3,2,1,0:T(8,128)S(1)}, u32[]{:S(2)}, u32[]{:S(2)}) collective-permute-start(f32[1,8,16,128]{3,2,1,0:T(8,128)S(1)} %get-tuple-element.49), channel_id=1, source_target_pairs={{4,0},{8,4},{12,8},{16,12},{20,16},{24,20},{28,24},{0,28},{5,1},{9... | collective-permute-start | bytes 196616 | tf_op jit(solution)/shard_map/ppermute | solution.py:20
  135.3 3.2 %collective-permute-start.34 = (f32[10,1,16,128]{3,2,1,0:T(8,128)S(1)}, f32[10,1,16,128]{3,2,1,0:T(8,128)S(1)}, u32[]{:S(2)}, u32[]{:S(2)}) collective-permute-start(f32[10,1,16,128]{3,2,1,0:T(8,128)S(1)} %get-tuple-element.34), channel_id=1, source_target_pairs={{1,0},{2,1},{3,2},{0,3},{5,4},{6,5},{7,6},{4,7},{9,8},{10,9},{11,1... | collective-permute-start | bytes 245768 | tf_op jit(solution)/shard_map/ppermute | solution.py:20
  136.2 4.3 %collective-permute-start.35 = (f32[10,1,16,128]{3,2,1,0:T(8,128)S(1)}, f32[10,1,16,128]{3,2,1,0:T(8,128)S(1)}, u32[]{:S(2)}, u32[]{:S(2)}) collective-permute-start(f32[10,1,16,128]{3,2,1,0:T(8,128)S(1)} %get-tuple-element.35), channel_id=1, source_target_pairs={{0,1},{1,2},{2,3},{3,0},{4,5},{5,6},{6,7},{7,4},{8,9},{9,10},{10,1... | collective-permute-start | bytes 245768 | tf_op jit(solution)/shard_map/ppermute | solution.py:19
  141.0 7.3 %collective-permute-start.37 = (f32[1,8,16,128]{3,2,1,0:T(8,128)S(1)}, f32[1,8,16,128]{3,2,1,0:T(8,128)S(1)}, u32[]{:S(2)}, u32[]{:S(2)}) collective-permute-start(f32[1,8,16,128]{3,2,1,0:T(8,128)S(1)} %get-tuple-element.42), channel_id=1, source_target_pairs={{0,4},{4,8},{8,12},{12,16},{16,20},{20,24},{24,28},{28,0},{1,5},{5... | collective-permute-start | bytes 196616 | tf_op jit(solution)/shard_map/ppermute | solution.py:19
  141.1 7.2 %collective-permute-start.36 = (f32[1,8,16,128]{3,2,1,0:T(8,128)S(1)}, f32[1,8,16,128]{3,2,1,0:T(8,128)S(1)}, u32[]{:S(2)}, u32[]{:S(2)}) collective-permute-start(f32[1,8,16,128]{3,2,1,0:T(8,128)S(1)} %get-tuple-element.43), channel_id=1, source_target_pairs={{4,0},{8,4},{12,8},{16,12},{20,16},{24,20},{28,24},{0,28},{5,1},{9... | collective-permute-start | bytes 196616 | tf_op jit(solution)/shard_map/ppermute | solution.py:20
  148.3 2.5 %collective-permute-start.38 = (f32[10,1,16,128]{3,2,1,0:T(8,128)S(1)}, f32[10,1,16,128]{3,2,1,0:T(8,128)S(1)}, u32[]{:S(2)}, u32[]{:S(2)}) collective-permute-start(f32[10,1,16,128]{3,2,1,0:T(8,128)S(1)} %get-tuple-element.32), channel_id=1, source_target_pairs={{1,0},{2,1},{3,2},{0,3},{5,4},{6,5},{7,6},{4,7},{9,8},{10,9},{11,1... | collective-permute-start | bytes 245768 | tf_op jit(solution)/shard_map/ppermute | solution.py:20
  148.4 4.2 %collective-permute-start.39 = (f32[10,1,16,128]{3,2,1,0:T(8,128)S(1)}, f32[10,1,16,128]{3,2,1,0:T(8,128)S(1)}, u32[]{:S(2)}, u32[]{:S(2)}) collective-permute-start(f32[10,1,16,128]{3,2,1,0:T(8,128)S(1)} %get-tuple-element.33), channel_id=1, source_target_pairs={{0,1},{1,2},{2,3},{3,0},{4,5},{5,6},{6,7},{7,4},{8,9},{9,10},{10,1... | collective-permute-start | bytes 245768 | tf_op jit(solution)/shard_map/ppermute | solution.py:19
  153.1 7.1 %collective-permute-start.41 = (f32[1,8,16,128]{3,2,1,0:T(8,128)S(1)}, f32[1,8,16,128]{3,2,1,0:T(8,128)S(1)}, u32[]{:S(2)}, u32[]{:S(2)}) collective-permute-start(f32[1,8,16,128]{3,2,1,0:T(8,128)S(1)} %get-tuple-element.40), channel_id=1, source_target_pairs={{0,4},{4,8},{8,12},{12,16},{16,20},{20,24},{24,28},{28,0},{1,5},{5... | collective-permute-start | bytes 196616 | tf_op jit(solution)/shard_map/ppermute | solution.py:19
  153.2 7.0 %collective-permute-start.40 = (f32[1,8,16,128]{3,2,1,0:T(8,128)S(1)}, f32[1,8,16,128]{3,2,1,0:T(8,128)S(1)}, u32[]{:S(2)}, u32[]{:S(2)}) collective-permute-start(f32[1,8,16,128]{3,2,1,0:T(8,128)S(1)} %get-tuple-element.41), channel_id=1, source_target_pairs={{4,0},{8,4},{12,8},{16,12},{20,16},{24,20},{28,24},{0,28},{5,1},{9... | collective-permute-start | bytes 196616 | tf_op jit(solution)/shard_map/ppermute | solution.py:20
  160.2 2.3 %collective-permute-start.42 = (f32[10,1,16,128]{3,2,1,0:T(8,128)S(1)}, f32[10,1,16,128]{3,2,1,0:T(8,128)S(1)}, u32[]{:S(2)}, u32[]{:S(2)}) collective-permute-start(f32[10,1,16,128]{3,2,1,0:T(8,128)S(1)} %get-tuple-element.30), channel_id=1, source_target_pairs={{1,0},{2,1},{3,2},{0,3},{5,4},{6,5},{7,6},{4,7},{9,8},{10,9},{11,1... | collective-permute-start | bytes 245768 | tf_op jit(solution)/shard_map/ppermute | solution.py:20
  160.3 4.4 %collective-permute-start.43 = (f32[10,1,16,128]{3,2,1,0:T(8,128)S(1)}, f32[10,1,16,128]{3,2,1,0:T(8,128)S(1)}, u32[]{:S(2)}, u32[]{:S(2)}) collective-permute-start(f32[10,1,16,128]{3,2,1,0:T(8,128)S(1)} %get-tuple-element.31), channel_id=1, source_target_pairs={{0,1},{1,2},{2,3},{3,0},{4,5},{5,6},{6,7},{7,4},{8,9},{9,10},{10,1... | collective-permute-start | bytes 245768 | tf_op jit(solution)/shard_map/ppermute | solution.py:19
where the time goes:
time: 166 us
  starting transfers between devices  70.2 us (42%)
  waiting for transfers between devices  60.8 us (37%)
  blocking collectives  12.5 us (8%)
  other arithmetic  9.63 us (6%)
  local copies, waits for them, and re-layouts  6.72 us (4%)
  matrix products  4.93 us (3%)
    ppermute x22, starting transfers between devices, padded(): after = lax.ppermute(initial, axis, down)  59.3 us
    ppermute x22, waiting for transfers between devices, padded(): before = lax.ppermute(last, axis, up)  43.3 us
    ppermute x22, waiting for transfers between devices, padded(): after = lax.ppermute(initial, axis, down)  17.6 us
    all_gather x2, blocking collectives, gathered_smooth(): lax.all_gather(pack_level(source, initial, diagonal), 'gy', axis=1, tiled...  12.5 us
    ppermute x22, starting transfers between devices, padded(): before = lax.ppermute(last, axis, up)  10.9 us
    dot_general x3, matrix products, prolong_local(): jnp.einsum('abkrj,abkij->abri', picked_lines, blocks, preferred_element_t...  4.93 us
  transfers between devices with their start and end apart: 44, of which 31 were waited for; matrix products, arithmetic and copies ran while one was open for 5% of the time, Pallas kernels for 0%

commit v1 on v0

--- a/solution.py
+++ b/solution.py
@@ -68,7 +68,7 @@
 
 def gathered_smooth(source, initial, diagonal):
     copies = source.shape[2]
-    gathered = lax.all_gather(pack_level(source, initial, diagonal), "gy", axis=1, tiled=True)
+    gathered = jnp.concatenate(jax.lax.all_gather(pack_level(source, initial, diagonal), "gy"), 1)
     return chebyshev(
         gathered[:, :, :copies],
         gathered[:, :, copies : 2 * copies],

time: 166 us -> 169 us (1.018)
  waiting for transfers between devices: 60.8 us -> 63.2 us
    ppermute x22, waiting for transfers between devices: 43.3 us -> 45.7 us  [padded(): before = lax.ppermute(last, axis, up)]
    ppermute x22, starting transfers between devices: 10.9 us -> 8.9 us  [padded(): before = lax.ppermute(last, axis, up)]
    ppermute x22, starting transfers between devices: 59.3 us -> 61.3 us  [padded(): after = lax.ppermute(initial, axis, down)]
  transfers between devices with their start and end apart: 44 -> 44, of which waited for: 31 -> 32; matrix products, arithmetic and copies ran while one was open for 5% -> 5% of each run, Pallas kernels for 0% -> 0%
where the time goes in v1:
time: 169 us; the launch traced here: 168 us
  starting transfers between devices  70.2 us (42%)
  waiting for transfers between devices  63.2 us (37%)
  blocking collectives  12 us (7%)
  other arithmetic  9.8 us (6%)
  local copies, waits for them, and re-layouts  6.85 us (4%)
  matrix products  4.93 us (3%)
    ppermute x22, starting transfers between devices, padded(): after = lax.ppermute(initial, axis, down)  61.3 us
    ppermute x22, waiting for transfers between devices, padded(): before = lax.ppermute(last, axis, up)  45.7 us
    ppermute x22, waiting for transfers between devices, padded(): after = lax.ppermute(initial, axis, down)  17.6 us
    all_gather x2, blocking collectives, gathered_smooth(): jax.lax.all_gather(pack_level(source, initial, diagonal), 'gy')  12 us
    ppermute x22, starting transfers between devices, padded(): before = lax.ppermute(last, axis, up)  8.9 us
    dot_general x3, matrix products, prolong_local(): jnp.einsum('abkrj,abkij->abri', picked_lines, blocks, preferred_element_t...  4.93 us
  transfers between devices with their start and end apart: 44, of which 32 were waited for; matrix products, arithmetic and copies ran while one was open for 5% of the time, Pallas kernels for 0%

profile of v1, /device:TPU:0, one launch (start us, length us, event | category | flops | bytes accessed | tf_op | source)
XLA Modules:
  0.0 168.3 jit_solution(4679848375615535220)
XLA Ops:
  0.6 0.8 pad_maximum_fusion.83
  1.5 6.2 %all-gather = f32[4,1,33,128]{3,1,2,0:T(1,128)S(1)} all-gather(f32[1,1,33,128]{3,1,2,0:T(1,128)S(1)} %pad_maximum_fusion.83), channel_id=2, replica_groups=mesh['gz'=8,'gy'=4] {'gy'}, dimensions={0}, use_global_device_ids=true | all-gather | bytes 84480 | tf_op jit(solution)/shard_map/all_gather | solution.py:71
  7.7 5.1 %collective-permute-start = (f32[1,4,16,128]{3,1,2,0:T(4,128)S(1)}, f32[1,4,16,128]{3,1,2,0:T(4,128)S(1)}, u32[]{:S(2)}, u32[]{:S(2)}) collective-permute-start(f32[1,4,16,128]{3,1,2,0:T(4,128)S(1)} %slice.670), channel_id=1, source_target_pairs={{4,0},{8,4},{12,8},{16,12},{20,16},{24,20},{28,24},{0,28},{5,1},{9... | collective-permute-start | bytes 98312 | tf_op jit(solution)/shard_map/ppermute | solution.py:20
  13.0 0.7 compare_select_fusion.10
  13.8 0.7 broadcast_multiply_fusion.5
  14.5 0.8 broadcast_multiply_fusion.3
  15.3 0.7 compare_select_fusion.5
  16.0 0.8 compare_select_fusion
  17.0 2.4 %collective-permute-done.1 = f32[1,4,16,128]{3,1,2,0:T(4,128)S(1)} collective-permute-done((f32[1,4,16,128]{3,1,2,0:T(4,128)S(1)}, f32[1,4,16,128]{3,1,2,0:T(4,128)S(1)}, u32[]{:S(2)}, u32[]{:S(2)}) %collective-permute-start.1) | collective-permute-done | bytes 32800 | tf_op jit(solution)/shard_map/ppermute | solution.py:19
  19.6 4.7 %collective-permute-start.2 = (f32[1,4,16,128]{3,1,2,0:T(4,128)S(1)}, f32[1,4,16,128]{3,1,2,0:T(4,128)S(1)}, u32[]{:S(2)}, u32[]{:S(2)}) collective-permute-start(f32[1,4,16,128]{3,1,2,0:T(4,128)S(1)} %get-tuple-element.32), channel_id=1, source_target_pairs={{4,0},{8,4},{12,8},{16,12},{20,16},{24,20},{28,24},{0,28},{5,1},{9... | collective-permute-start | bytes 98312 | tf_op jit(solution)/shard_map/ppermute | solution.py:20
  24.5 1.7 collective-permute-done.3
  26.4 4.8 %collective-permute-start.4 = (f32[1,4,16,128]{3,1,2,0:T(4,128)S(1)}, f32[1,4,16,128]{3,1,2,0:T(4,128)S(1)}, u32[]{:S(2)}, u32[]{:S(2)}) collective-permute-start(f32[1,4,16,128]{3,1,2,0:T(4,128)S(1)} %get-tuple-element.30), channel_id=1, source_target_pairs={{4,0},{8,4},{12,8},{16,12},{20,16},{24,20},{28,24},{0,28},{5,1},{9... | collective-permute-start | bytes 98312 | tf_op jit(solution)/shard_map/ppermute | solution.py:20
  31.4 1.6 collective-permute-done.5
  33.1 4.8 %collective-permute-start.7 = (bf16[1,4,16,128]{3,1,2,0:T(4,128)(2,1)S(1)}, bf16[1,4,16,128]{3,1,2,0:T(4,128)(2,1)S(1)}, u32[]{:S(2)}, u32[]{:S(2)}) collective-permute-start(bf16[1,4,16,128]{3,1,2,0:T(4,128)(2,1)S(1)} %get-tuple-element.28), channel_id=1, source_target_pairs={{4,0},{8,4},{12,8},{16,12},{20,16},{24,20},{28,24},{0,28},{5,1},{9... | collective-permute-start | bytes 49160 | tf_op jit(solution)/shard_map/ppermute | solution.py:20
  38.2 1.2 collective-permute-done.7
  39.4 5.0 %collective-permute-done.6 = bf16[1,4,16,128]{3,1,2,0:T(4,128)(2,1)S(1)} collective-permute-done((bf16[1,4,16,128]{3,1,2,0:T(4,128)(2,1)S(1)}, bf16[1,4,16,128]{3,1,2,0:T(4,128)(2,1)S(1)}, u32[]{:S(2)}, u32[]{:S(2)}) %collective-permute-start.6) | collective-permute-done | bytes 16416 | tf_op jit(solution)/shard_map/ppermute | solution.py:19
  45.2 1.1 fusion.2
  46.3 0.8 pad_maximum_fusion.69
  47.1 5.8 %all-gather.1 = f32[8,2,33,128]{3,1,2,0:T(2,128)S(1)} all-gather(f32[2,2,33,128]{3,1,2,0:T(2,128)S(1)} %copy.54), channel_id=3, replica_groups=mesh['gz'=8,'gy'=4] {'gy'}, dimensions={0}, use_global_device_ids=true | all-gather | bytes 337920 | tf_op jit(solution)/shard_map/all_gather | solution.py:71
  53.3 2.0 %collective-permute-start.9 = (f32[1,8,16,128]{3,2,1,0:T(8,128)S(1)}, f32[1,8,16,128]{3,2,1,0:T(8,128)S(1)}, u32[]{:S(2)}, u32[]{:S(2)}) collective-permute-start(f32[1,8,16,128]{3,2,1,0:T(8,128)S(1)} %get-tuple-element.59), channel_id=1, source_target_pairs={{0,4},{4,8},{8,12},{12,16},{16,20},{20,24},{24,28},{28,0},{1,5},{5... | collective-permute-start | bytes 196616 | tf_op jit(solution)/shard_map/ppermute | solution.py:19
  55.3 2.3 %collective-permute-done.8 = f32[1,8,16,128]{3,2,1,0:T(8,128)S(1)} collective-permute-done((f32[1,8,16,128]{3,2,1,0:T(8,128)S(1)}, f32[1,8,16,128]{3,2,1,0:T(8,128)S(1)}, u32[]{:S(2)}, u32[]{:S(2)}) %collective-permute-start.8) | collective-permute-done | bytes 65568 | tf_op jit(solution)/shard_map/ppermute | solution.py:20
  57.6 2.8 %collective-permute-done.9 = f32[1,8,16,128]{3,2,1,0:T(8,128)S(1)} collective-permute-done((f32[1,8,16,128]{3,2,1,0:T(8,128)S(1)}, f32[1,8,16,128]{3,2,1,0:T(8,128)S(1)}, u32[]{:S(2)}, u32[]{:S(2)}) %collective-permute-start.9) | collective-permute-done | bytes 65568 | tf_op jit(solution)/shard_map/ppermute | solution.py:19
  61.1 1.8 %collective-permute-start.11 = (f32[1,8,16,128]{3,2,1,0:T(8,128)S(1)}, f32[1,8,16,128]{3,2,1,0:T(8,128)S(1)}, u32[]{:S(2)}, u32[]{:S(2)}) collective-permute-start(f32[1,8,16,128]{3,2,1,0:T(8,128)S(1)} %get-tuple-element.103), channel_id=1, source_target_pairs={{0,4},{4,8},{8,12},{12,16},{16,20},{20,24},{24,28},{28,0},{1,5},{5... | collective-permute-start | bytes 196616 | tf_op jit(solution)/shard_map/ppermute | solution.py:19
  62.9 2.2 %collective-permute-done.10 = f32[1,8,16,128]{3,2,1,0:T(8,128)S(1)} collective-permute-done((f32[1,8,16,128]{3,2,1,0:T(8,128)S(1)}, f32[1,8,16,128]{3,2,1,0:T(8,128)S(1)}, u32[]{:S(2)}, u32[]{:S(2)}) %collective-permute-start.10) | collective-permute-done | bytes 65568 | tf_op jit(solution)/shard_map/ppermute | solution.py:20
  65.1 2.9 %collective-permute-done.11 = f32[1,8,16,128]{3,2,1,0:T(8,128)S(1)} collective-permute-done((f32[1,8,16,128]{3,2,1,0:T(8,128)S(1)}, f32[1,8,16,128]{3,2,1,0:T(8,128)S(1)}, u32[]{:S(2)}, u32[]{:S(2)}) %collective-permute-start.11) | collective-permute-done | bytes 65568 | tf_op jit(solution)/shard_map/ppermute | solution.py:19
  68.5 2.0 %collective-permute-start.13 = (f32[1,8,16,128]{3,2,1,0:T(8,128)S(1)}, f32[1,8,16,128]{3,2,1,0:T(8,128)S(1)}, u32[]{:S(2)}, u32[]{:S(2)}) collective-permute-start(f32[1,8,16,128]{3,2,1,0:T(8,128)S(1)} %get-tuple-element.93), channel_id=1, source_target_pairs={{0,4},{4,8},{8,12},{12,16},{16,20},{20,24},{24,28},{28,0},{1,5},{5... | collective-permute-start | bytes 196616 | tf_op jit(solution)/shard_map/ppermute | solution.py:19
  70.5 2.9 %collective-permute-done.12 = f32[1,8,16,128]{3,2,1,0:T(8,128)S(1)} collective-permute-done((f32[1,8,16,128]{3,2,1,0:T(8,128)S(1)}, f32[1,8,16,128]{3,2,1,0:T(8,128)S(1)}, u32[]{:S(2)}, u32[]{:S(2)}) %collective-permute-start.12) | collective-permute-done | bytes 65568 | tf_op jit(solution)/shard_map/ppermute | solution.py:20
  73.5 2.1 %collective-permute-done.13 = f32[1,8,16,128]{3,2,1,0:T(8,128)S(1)} collective-permute-done((f32[1,8,16,128]{3,2,1,0:T(8,128)S(1)}, f32[1,8,16,128]{3,2,1,0:T(8,128)S(1)}, u32[]{:S(2)}, u32[]{:S(2)}) %collective-permute-start.13) | collective-permute-done | bytes 65568 | tf_op jit(solution)/shard_map/ppermute | solution.py:19
  75.8 4.7 %collective-permute-start.15 = (bf16[1,8,16,128]{3,2,1,0:T(8,128)(2,1)S(1)}, bf16[1,8,16,128]{3,2,1,0:T(8,128)(2,1)S(1)}, u32[]{:S(2)}, u32[]{:S(2)}) collective-permute-start(bf16[1,8,16,128]{3,2,1,0:T(8,128)(2,1)S(1)} %get-tuple-element.125), channel_id=1, source_target_pairs={{4,0},{8,4},{12,8},{16,12},{20,16},{24,20},{28,24},{0,28},{5,1},{9... | collective-permute-start | bytes 98312 | tf_op jit(solution)/shard_map/ppermute | solution.py:20
  80.5 1.9 %collective-permute-done.14 = bf16[1,8,16,128]{3,2,1,0:T(8,128)(2,1)S(1)} collective-permute-done((bf16[1,8,16,128]{3,2,1,0:T(8,128)(2,1)S(1)}, bf16[1,8,16,128]{3,2,1,0:T(8,128)(2,1)S(1)}, u32[]{:S(2)}, u32[]{:S(2)}) %collective-permute-start.14) | collective-permute-done | bytes 32800 | tf_op jit(solution)/shard_map/ppermute | solution.py:19
  83.5 4.9 %collective-permute-start.16 = (f32[1,4,16,128]{3,2,1,0:T(8,128)S(1)}, f32[1,4,16,128]{3,2,1,0:T(8,128)S(1)}, u32[]{:S(2)}, u32[]{:S(2)}) collective-permute-start(f32[1,4,16,128]{3,2,1,0:T(8,128)S(1)} %get-tuple-element.87), channel_id=1, source_target_pairs={{4,0},{8,4},{12,8},{16,12},{20,16},{24,20},{28,24},{0,28},{5,1},{9... | collective-permute-start | bytes 98312 | tf_op jit(solution)/shard_map/ppermute | solution.py:20
  88.4 1.7 %collective-permute-done.17 = f32[1,4,16,128]{3,2,1,0:T(8,128)S(1)} collective-permute-done((f32[1,4,16,128]{3,2,1,0:T(8,128)S(1)}, f32[1,4,16,128]{3,2,1,0:T(8,128)S(1)}, u32[]{:S(2)}, u32[]{:S(2)}) %collective-permute-start.17) | collective-permute-done | bytes 32800 | tf_op jit(solution)/shard_map/ppermute | solution.py:19
  90.9 1.1 collective-permute-done.18
  92.0 2.3 %collective-permute-done.19 = f32[6,1,16,128]{3,2,1,0:T(8,128)S(1)} collective-permute-done((f32[6,1,16,128]{3,2,1,0:T(8,128)S(1)}, f32[6,1,16,128]{3,2,1,0:T(8,128)S(1)}, u32[]{:S(2)}, u32[]{:S(2)}) %collective-permute-start.19) | collective-permute-done | bytes 49184 | tf_op jit(solution)/shard_map/ppermute | solution.py:19
  94.6 4.8 %collective-permute-start.20 = (f32[1,4,16,128]{3,2,1,0:T(8,128)S(1)}, f32[1,4,16,128]{3,2,1,0:T(8,128)S(1)}, u32[]{:S(2)}, u32[]{:S(2)}) collective-permute-start(f32[1,4,16,128]{3,2,1,0:T(8,128)S(1)} %get-tuple-element.81), channel_id=1, source_target_pairs={{4,0},{8,4},{12,8},{16,12},{20,16},{24,20},{28,24},{0,28},{5,1},{9... | collective-permute-start | bytes 98312 | tf_op jit(solution)/shard_map/ppermute | solution.py:20
  99.5 1.7 %collective-permute-done.21 = f32[1,4,16,128]{3,2,1,0:T(8,128)S(1)} collective-permute-done((f32[1,4,16,128]{3,2,1,0:T(8,128)S(1)}, f32[1,4,16,128]{3,2,1,0:T(8,128)S(1)}, u32[]{:S(2)}, u32[]{:S(2)}) %collective-permute-start.21) | collective-permute-done | bytes 32800 | tf_op jit(solution)/shard_map/ppermute | solution.py:19
  101.9 1.1 collective-permute-done.22
  103.1 1.8 %collective-permute-done.23 = f32[6,1,16,128]{3,2,1,0:T(8,128)S(1)} collective-permute-done((f32[6,1,16,128]{3,2,1,0:T(8,128)S(1)}, f32[6,1,16,128]{3,2,1,0:T(8,128)S(1)}, u32[]{:S(2)}, u32[]{:S(2)}) %collective-permute-start.23) | collective-permute-done | bytes 49184 | tf_op jit(solution)/shard_map/ppermute | solution.py:19
  105.1 4.8 %collective-permute-start.24 = (f32[1,4,16,128]{3,2,1,0:T(8,128)S(1)}, f32[1,4,16,128]{3,2,1,0:T(8,128)S(1)}, u32[]{:S(2)}, u32[]{:S(2)}) collective-permute-start(f32[1,4,16,128]{3,2,1,0:T(8,128)S(1)} %get-tuple-element.75), channel_id=1, source_target_pairs={{4,0},{8,4},{12,8},{16,12},{20,16},{24,20},{28,24},{0,28},{5,1},{9... | collective-permute-start | bytes 98312 | tf_op jit(solution)/shard_map/ppermute | solution.py:20
  110.1 1.7 %collective-permute-done.25 = f32[1,4,16,128]{3,2,1,0:T(8,128)S(1)} collective-permute-done((f32[1,4,16,128]{3,2,1,0:T(8,128)S(1)}, f32[1,4,16,128]{3,2,1,0:T(8,128)S(1)}, u32[]{:S(2)}, u32[]{:S(2)}) %collective-permute-start.25) | collective-permute-done | bytes 32800 | tf_op jit(solution)/shard_map/ppermute | solution.py:19
  112.5 1.1 collective-permute-done.26
  113.6 1.9 %collective-permute-done.27 = f32[6,1,16,128]{3,2,1,0:T(8,128)S(1)} collective-permute-done((f32[6,1,16,128]{3,2,1,0:T(8,128)S(1)}, f32[6,1,16,128]{3,2,1,0:T(8,128)S(1)}, u32[]{:S(2)}, u32[]{:S(2)}) %collective-permute-start.27) | collective-permute-done | bytes 49184 | tf_op jit(solution)/shard_map/ppermute | solution.py:19
  115.5 0.8 fusion.100
  116.3 4.8 %collective-permute-start.29 = (bf16[1,4,16,128]{3,2,1,0:T(8,128)(2,1)S(1)}, bf16[1,4,16,128]{3,2,1,0:T(8,128)(2,1)S(1)}, u32[]{:S(2)}, u32[]{:S(2)}) collective-permute-start(bf16[1,4,16,128]{3,2,1,0:T(8,128)(2,1)S(1)} %get-tuple-element.123), channel_id=1, source_target_pairs={{4,0},{8,4},{12,8},{16,12},{20,16},{24,20},{28,24},{0,28},{5,1},{9... | collective-permute-start | bytes 49160 | tf_op jit(solution)/shard_map/ppermute | solution.py:20
  121.7 1.1 collective-permute-done.28
  122.9 1.7 %collective-permute-start.31 = (bf16[6,1,16,128]{3,2,1,0:T(8,128)(2,1)S(1)}, bf16[6,1,16,128]{3,2,1,0:T(8,128)(2,1)S(1)}, u32[]{:S(2)}, u32[]{:S(2)}) collective-permute-start(bf16[6,1,16,128]{3,2,1,0:T(8,128)(2,1)S(1)} %get-tuple-element.113), channel_id=1, source_target_pairs={{1,0},{2,1},{3,2},{0,3},{5,4},{6,5},{7,6},{4,7},{9,8},{10,9},{11,1... | collective-permute-start | bytes 73736 | tf_op jit(solution)/shard_map/ppermute | solution.py:20
  124.6 0.6 constant_dynamic-slice_fusion.1
  125.2 0.9 collective-permute-done.30
  126.2 0.7 gather_fusion.2
  126.9 3.4 %fusion = f32[8,8,16,128]{3,2,1,0:T(8,128)S(1)} fusion(f32[8,8,16,128]{3,2,1,0:T(8,128)S(1)} %copy-done.2, bf16[8,8,2,16,128]{4,3,2,1,0:T(8,128)(2,1)S(1)} %bitcast.65, bf16[8,8,2,128,128]{4,3,2,1,0:T(8,128)(2,1)} %param.30), kind=kOutput, calls=%fused_computation.4 | convolution fusion | flops 67239936 | bytes 5767168 | tf_op jit(solution)/shard_map/abkrj,abkij->abri/dot_general | solution.py:91
  130.4 4.8 %collective-permute-start.32 = (f32[1,8,16,128]{3,2,1,0:T(8,128)S(1)}, f32[1,8,16,128]{3,2,1,0:T(8,128)S(1)}, u32[]{:S(2)}, u32[]{:S(2)}) collective-permute-start(f32[1,8,16,128]{3,2,1,0:T(8,128)S(1)} %get-tuple-element.53), channel_id=1, source_target_pairs={{4,0},{8,4},{12,8},{16,12},{20,16},{24,20},{28,24},{0,28},{5,1},{9... | collective-permute-start | bytes 196616 | tf_op jit(solution)/shard_map/ppermute | solution.py:20
  135.4 2.3 %collective-permute-done.33 = f32[1,8,16,128]{3,2,1,0:T(8,128)S(1)} collective-permute-done((f32[1,8,16,128]{3,2,1,0:T(8,128)S(1)}, f32[1,8,16,128]{3,2,1,0:T(8,128)S(1)}, u32[]{:S(2)}, u32[]{:S(2)}) %collective-permute-start.33) | collective-permute-done | bytes 65568 | tf_op jit(solution)/shard_map/ppermute | solution.py:19
  137.7 0.9 collective-permute-start.34
  138.8 2.2 %collective-permute-done.34 = f32[10,1,16,128]{3,2,1,0:T(8,128)S(1)} collective-permute-done((f32[10,1,16,128]{3,2,1,0:T(8,128)S(1)}, f32[10,1,16,128]{3,2,1,0:T(8,128)S(1)}, u32[]{:S(2)}, u32[]{:S(2)}) %collective-permute-start.34) | collective-permute-done | bytes 81952 | tf_op jit(solution)/shard_map/ppermute | solution.py:20
  140.9 2.0 %collective-permute-done.35 = f32[10,1,16,128]{3,2,1,0:T(8,128)S(1)} collective-permute-done((f32[10,1,16,128]{3,2,1,0:T(8,128)S(1)}, f32[10,1,16,128]{3,2,1,0:T(8,128)S(1)}, u32[]{:S(2)}, u32[]{:S(2)}) %collective-permute-start.35) | collective-permute-done | bytes 81952 | tf_op jit(solution)/shard_map/ppermute | solution.py:19
  143.4 5.0 %collective-permute-start.36 = (f32[1,8,16,128]{3,2,1,0:T(8,128)S(1)}, f32[1,8,16,128]{3,2,1,0:T(8,128)S(1)}, u32[]{:S(2)}, u32[]{:S(2)}) collective-permute-start(f32[1,8,16,128]{3,2,1,0:T(8,128)S(1)} %get-tuple-element.47), channel_id=1, source_target_pairs={{4,0},{8,4},{12,8},{16,12},{20,16},{24,20},{28,24},{0,28},{5,1},{9... | collective-permute-start | bytes 196616 | tf_op jit(solution)/shard_map/ppermute | solution.py:20
  148.7 2.0 %collective-permute-done.37 = f32[1,8,16,128]{3,2,1,0:T(8,128)S(1)} collective-permute-done((f32[1,8,16,128]{3,2,1,0:T(8,128)S(1)}, f32[1,8,16,128]{3,2,1,0:T(8,128)S(1)}, u32[]{:S(2)}, u32[]{:S(2)}) %collective-permute-start.37) | collective-permute-done | bytes 65568 | tf_op jit(solution)/shard_map/ppermute | solution.py:19
  151.4 1.7 %collective-permute-done.38 = f32[10,1,16,128]{3,2,1,0:T(8,128)S(1)} collective-permute-done((f32[10,1,16,128]{3,2,1,0:T(8,128)S(1)}, f32[10,1,16,128]{3,2,1,0:T(8,128)S(1)}, u32[]{:S(2)}, u32[]{:S(2)}) %collective-permute-start.38) | collective-permute-done | bytes 81952 | tf_op jit(solution)/shard_map/ppermute | solution.py:20
  153.1 1.8 %collective-permute-done.39 = f32[10,1,16,128]{3,2,1,0:T(8,128)S(1)} collective-permute-done((f32[10,1,16,128]{3,2,1,0:T(8,128)S(1)}, f32[10,1,16,128]{3,2,1,0:T(8,128)S(1)}, u32[]{:S(2)}, u32[]{:S(2)}) %collective-permute-start.39) | collective-permute-done | bytes 81952 | tf_op jit(solution)/shard_map/ppermute | solution.py:19
  155.5 4.8 %collective-permute-start.40 = (f32[1,8,16,128]{3,2,1,0:T(8,128)S(1)}, f32[1,8,16,128]{3,2,1,0:T(8,128)S(1)}, u32[]{:S(2)}, u32[]{:S(2)}) collective-permute-start(f32[1,8,16,128]{3,2,1,0:T(8,128)S(1)} %get-tuple-element.45), channel_id=1, source_target_pairs={{4,0},{8,4},{12,8},{16,12},{20,16},{24,20},{28,24},{0,28},{5,1},{9... | collective-permute-start | bytes 196616 | tf_op jit(solution)/shard_map/ppermute | solution.py:20
  160.6 2.0 %collective-permute-done.41 = f32[1,8,16,128]{3,2,1,0:T(8,128)S(1)} collective-permute-done((f32[1,8,16,128]{3,2,1,0:T(8,128)S(1)}, f32[1,8,16,128]{3,2,1,0:T(8,128)S(1)}, u32[]{:S(2)}, u32[]{:S(2)}) %collective-permute-start.41) | collective-permute-done | bytes 65568 | tf_op jit(solution)/shard_map/ppermute | solution.py:19
  163.3 1.5 collective-permute-done.42
  164.9 2.1 %collective-permute-done.43 = f32[10,1,16,128]{3,2,1,0:T(8,128)S(1)} collective-permute-done((f32[10,1,16,128]{3,2,1,0:T(8,128)S(1)}, f32[10,1,16,128]{3,2,1,0:T(8,128)S(1)}, u32[]{:S(2)}, u32[]{:S(2)}) %collective-permute-start.43) | collective-permute-done | bytes 81952 | tf_op jit(solution)/shard_map/ppermute | solution.py:19
  167.0 1.3 fusion.9
  (140 shorter events, 12.1 us)
Async XLA Ops:
  0.6 82.4 %copy-start = (bf16[4,4,2,128,128]{4,3,2,1,0:T(8,128)(2,1)S(1)}, bf16[4,4,2,128,128]{4,3,2,1,0:T(8,128)(2,1)}, u32[]{:S(2)}) copy-start(bf16[4,4,2,128,128]{4,3,2,1,0:T(8,128)(2,1)} %param.31) | copy-start | bytes 3145732
  7.7 9.3 %collective-permute-start = (f32[1,4,16,128]{3,1,2,0:T(4,128)S(1)}, f32[1,4,16,128]{3,1,2,0:T(4,128)S(1)}, u32[]{:S(2)}, u32[]{:S(2)}) collective-permute-start(f32[1,4,16,128]{3,1,2,0:T(4,128)S(1)} %slice.670), channel_id=1, source_target_pairs={{4,0},{8,4},{12,8},{16,12},{20,16},{24,20},{28,24},{0,28},{5,1},{9... | collective-permute-start | bytes 98312 | tf_op jit(solution)/shard_map/ppermute | solution.py:20
  12.8 6.6 %collective-permute-start.1 = (f32[1,4,16,128]{3,1,2,0:T(4,128)S(1)}, f32[1,4,16,128]{3,1,2,0:T(4,128)S(1)}, u32[]{:S(2)}, u32[]{:S(2)}) collective-permute-start(f32[1,4,16,128]{3,1,2,0:T(4,128)S(1)} %slice.670), channel_id=1, source_target_pairs={{0,4},{4,8},{8,12},{12,16},{16,20},{20,24},{24,28},{28,0},{1,5},{5... | collective-permute-start | bytes 98312 | tf_op jit(solution)/shard_map/ppermute | solution.py:19
  19.5 6.7 %collective-permute-start.3 = (f32[1,4,16,128]{3,1,2,0:T(4,128)S(1)}, f32[1,4,16,128]{3,1,2,0:T(4,128)S(1)}, u32[]{:S(2)}, u32[]{:S(2)}) collective-permute-start(f32[1,4,16,128]{3,1,2,0:T(4,128)S(1)} %get-tuple-element.32), channel_id=1, source_target_pairs={{0,4},{4,8},{8,12},{12,16},{16,20},{20,24},{24,28},{28,0},{1,5},{5... | collective-permute-start | bytes 98312 | tf_op jit(solution)/shard_map/ppermute | solution.py:19
  19.6 6.6 %collective-permute-start.2 = (f32[1,4,16,128]{3,1,2,0:T(4,128)S(1)}, f32[1,4,16,128]{3,1,2,0:T(4,128)S(1)}, u32[]{:S(2)}, u32[]{:S(2)}) collective-permute-start(f32[1,4,16,128]{3,1,2,0:T(4,128)S(1)} %get-tuple-element.32), channel_id=1, source_target_pairs={{4,0},{8,4},{12,8},{16,12},{20,16},{24,20},{28,24},{0,28},{5,1},{9... | collective-permute-start | bytes 98312 | tf_op jit(solution)/shard_map/ppermute | solution.py:20
  26.3 6.7 %collective-permute-start.5 = (f32[1,4,16,128]{3,1,2,0:T(4,128)S(1)}, f32[1,4,16,128]{3,1,2,0:T(4,128)S(1)}, u32[]{:S(2)}, u32[]{:S(2)}) collective-permute-start(f32[1,4,16,128]{3,1,2,0:T(4,128)S(1)} %get-tuple-element.30), channel_id=1, source_target_pairs={{0,4},{4,8},{8,12},{12,16},{16,20},{20,24},{24,28},{28,0},{1,5},{5... | collective-permute-start | bytes 98312 | tf_op jit(solution)/shard_map/ppermute | solution.py:19
  26.4 6.6 %collective-permute-start.4 = (f32[1,4,16,128]{3,1,2,0:T(4,128)S(1)}, f32[1,4,16,128]{3,1,2,0:T(4,128)S(1)}, u32[]{:S(2)}, u32[]{:S(2)}) collective-permute-start(f32[1,4,16,128]{3,1,2,0:T(4,128)S(1)} %get-tuple-element.30), channel_id=1, source_target_pairs={{4,0},{8,4},{12,8},{16,12},{20,16},{24,20},{28,24},{0,28},{5,1},{9... | collective-permute-start | bytes 98312 | tf_op jit(solution)/shard_map/ppermute | solution.py:20
  33.1 6.3 %collective-permute-start.7 = (bf16[1,4,16,128]{3,1,2,0:T(4,128)(2,1)S(1)}, bf16[1,4,16,128]{3,1,2,0:T(4,128)(2,1)S(1)}, u32[]{:S(2)}, u32[]{:S(2)}) collective-permute-start(bf16[1,4,16,128]{3,1,2,0:T(4,128)(2,1)S(1)} %get-tuple-element.28), channel_id=1, source_target_pairs={{4,0},{8,4},{12,8},{16,12},{20,16},{24,20},{28,24},{0,28},{5,1},{9... | collective-permute-start | bytes 49160 | tf_op jit(solution)/shard_map/ppermute | solution.py:20
  37.9 6.4 %collective-permute-start.6 = (bf16[1,4,16,128]{3,1,2,0:T(4,128)(2,1)S(1)}, bf16[1,4,16,128]{3,1,2,0:T(4,128)(2,1)S(1)}, u32[]{:S(2)}, u32[]{:S(2)}) collective-permute-start(bf16[1,4,16,128]{3,1,2,0:T(4,128)(2,1)S(1)} %get-tuple-element.28), channel_id=1, source_target_pairs={{0,4},{4,8},{8,12},{12,16},{16,20},{20,24},{24,28},{28,0},{1,5},{5... | collective-permute-start | bytes 49160 | tf_op jit(solution)/shard_map/ppermute | solution.py:19
  53.2 4.4 %collective-permute-start.8 = (f32[1,8,16,128]{3,2,1,0:T(8,128)S(1)}, f32[1,8,16,128]{3,2,1,0:T(8,128)S(1)}, u32[]{:S(2)}, u32[]{:S(2)}) collective-permute-start(f32[1,8,16,128]{3,2,1,0:T(8,128)S(1)} %get-tuple-element.58), channel_id=1, source_target_pairs={{4,0},{8,4},{12,8},{16,12},{20,16},{24,20},{28,24},{0,28},{5,1},{9... | collective-permute-start | bytes 196616 | tf_op jit(solution)/shard_map/ppermute | solution.py:20
  53.3 7.1 %collective-permute-start.9 = (f32[1,8,16,128]{3,2,1,0:T(8,128)S(1)}, f32[1,8,16,128]{3,2,1,0:T(8,128)S(1)}, u32[]{:S(2)}, u32[]{:S(2)}) collective-permute-start(f32[1,8,16,128]{3,2,1,0:T(8,128)S(1)} %get-tuple-element.59), channel_id=1, source_target_pairs={{0,4},{4,8},{8,12},{12,16},{16,20},{20,24},{24,28},{28,0},{1,5},{5... | collective-permute-start | bytes 196616 | tf_op jit(solution)/shard_map/ppermute | solution.py:19
  60.4 22.6 %copy-start.4 = (f32[4,4,16,128]{3,2,1,0:T(8,128)S(1)}, f32[4,4,16,128]{3,2,1,0:T(8,128)}, u32[]{:S(2)}) copy-start(f32[4,4,16,128]{3,2,1,0:T(8,128)} %param.23) | copy-start | bytes 393220
  60.8 4.3 %collective-permute-start.10 = (f32[1,8,16,128]{3,2,1,0:T(8,128)S(1)}, f32[1,8,16,128]{3,2,1,0:T(8,128)S(1)}, u32[]{:S(2)}, u32[]{:S(2)}) collective-permute-start(f32[1,8,16,128]{3,2,1,0:T(8,128)S(1)} %get-tuple-element.102), channel_id=1, source_target_pairs={{4,0},{8,4},{12,8},{16,12},{20,16},{24,20},{28,24},{0,28},{5,1},{9... | collective-permute-start | bytes 196616 | tf_op jit(solution)/shard_map/ppermute | solution.py:20
  61.1 7.0 %collective-permute-start.11 = (f32[1,8,16,128]{3,2,1,0:T(8,128)S(1)}, f32[1,8,16,128]{3,2,1,0:T(8,128)S(1)}, u32[]{:S(2)}, u32[]{:S(2)}) collective-permute-start(f32[1,8,16,128]{3,2,1,0:T(8,128)S(1)} %get-tuple-element.103), channel_id=1, source_target_pairs={{0,4},{4,8},{8,12},{12,16},{16,20},{20,24},{24,28},{28,0},{1,5},{5... | collective-permute-start | bytes 196616 | tf_op jit(solution)/shard_map/ppermute | solution.py:19
  68.0 26.3 %copy-start.3 = (f32[4,4,16,128]{3,2,1,0:T(8,128)S(1)}, f32[4,4,16,128]{3,2,1,0:T(8,128)}, u32[]{:S(2)}) copy-start(f32[4,4,16,128]{3,2,1,0:T(8,128)} %param.19) | copy-start | bytes 393220
  68.4 5.0 %collective-permute-start.12 = (f32[1,8,16,128]{3,2,1,0:T(8,128)S(1)}, f32[1,8,16,128]{3,2,1,0:T(8,128)S(1)}, u32[]{:S(2)}, u32[]{:S(2)}) collective-permute-start(f32[1,8,16,128]{3,2,1,0:T(8,128)S(1)} %get-tuple-element.92), channel_id=1, source_target_pairs={{4,0},{8,4},{12,8},{16,12},{20,16},{24,20},{28,24},{0,28},{5,1},{9... | collective-permute-start | bytes 196616 | tf_op jit(solution)/shard_map/ppermute | solution.py:20
  68.5 7.0 %collective-permute-start.13 = (f32[1,8,16,128]{3,2,1,0:T(8,128)S(1)}, f32[1,8,16,128]{3,2,1,0:T(8,128)S(1)}, u32[]{:S(2)}, u32[]{:S(2)}) collective-permute-start(f32[1,8,16,128]{3,2,1,0:T(8,128)S(1)} %get-tuple-element.93), channel_id=1, source_target_pairs={{0,4},{4,8},{8,12},{12,16},{16,20},{20,24},{24,28},{28,0},{1,5},{5... | collective-permute-start | bytes 196616 | tf_op jit(solution)/shard_map/ppermute | solution.py:19
  75.7 6.7 %collective-permute-start.14 = (bf16[1,8,16,128]{3,2,1,0:T(8,128)(2,1)S(1)}, bf16[1,8,16,128]{3,2,1,0:T(8,128)(2,1)S(1)}, u32[]{:S(2)}, u32[]{:S(2)}) collective-permute-start(bf16[1,8,16,128]{3,2,1,0:T(8,128)(2,1)S(1)} %get-tuple-element.124), channel_id=1, source_target_pairs={{0,4},{4,8},{8,12},{12,16},{16,20},{20,24},{24,28},{28,0},{1,5},{5... | collective-permute-start | bytes 98312 | tf_op jit(solution)/shard_map/ppermute | solution.py:19
  75.8 6.6 %collective-permute-start.15 = (bf16[1,8,16,128]{3,2,1,0:T(8,128)(2,1)S(1)}, bf16[1,8,16,128]{3,2,1,0:T(8,128)(2,1)S(1)}, u32[]{:S(2)}, u32[]{:S(2)}) collective-permute-start(bf16[1,8,16,128]{3,2,1,0:T(8,128)(2,1)S(1)} %get-tuple-element.125), channel_id=1, source_target_pairs={{4,0},{8,4},{12,8},{16,12},{20,16},{24,20},{28,24},{0,28},{5,1},{9... | collective-permute-start | bytes 98312 | tf_op jit(solution)/shard_map/ppermute | solution.py:20
  83.4 6.8 %collective-permute-start.17 = (f32[1,4,16,128]{3,2,1,0:T(8,128)S(1)}, f32[1,4,16,128]{3,2,1,0:T(8,128)S(1)}, u32[]{:S(2)}, u32[]{:S(2)}) collective-permute-start(f32[1,4,16,128]{3,2,1,0:T(8,128)S(1)} %get-tuple-element.86), channel_id=1, source_target_pairs={{0,4},{4,8},{8,12},{12,16},{16,20},{20,24},{24,28},{28,0},{1,5},{5... | collective-permute-start | bytes 98312 | tf_op jit(solution)/shard_map/ppermute | solution.py:19
  83.5 6.7 %collective-permute-start.16 = (f32[1,4,16,128]{3,2,1,0:T(8,128)S(1)}, f32[1,4,16,128]{3,2,1,0:T(8,128)S(1)}, u32[]{:S(2)}, u32[]{:S(2)}) collective-permute-start(f32[1,4,16,128]{3,2,1,0:T(8,128)S(1)} %get-tuple-element.87), channel_id=1, source_target_pairs={{4,0},{8,4},{12,8},{16,12},{20,16},{24,20},{28,24},{0,28},{5,1},{9... | collective-permute-start | bytes 98312 | tf_op jit(solution)/shard_map/ppermute | solution.py:20
  90.2 1.8 %collective-permute-start.18 = (f32[6,1,16,128]{3,2,1,0:T(8,128)S(1)}, f32[6,1,16,128]{3,2,1,0:T(8,128)S(1)}, u32[]{:S(2)}, u32[]{:S(2)}) collective-permute-start(f32[6,1,16,128]{3,2,1,0:T(8,128)S(1)} %get-tuple-element.72), channel_id=1, source_target_pairs={{1,0},{2,1},{3,2},{0,3},{5,4},{6,5},{7,6},{4,7},{9,8},{10,9},{11,1... | collective-permute-start | bytes 147464 | tf_op jit(solution)/shard_map/ppermute | solution.py:20
  90.3 4.1 %collective-permute-start.19 = (f32[6,1,16,128]{3,2,1,0:T(8,128)S(1)}, f32[6,1,16,128]{3,2,1,0:T(8,128)S(1)}, u32[]{:S(2)}, u32[]{:S(2)}) collective-permute-start(f32[6,1,16,128]{3,2,1,0:T(8,128)S(1)} %get-tuple-element.73), channel_id=1, source_target_pairs={{0,1},{1,2},{2,3},{3,0},{4,5},{5,6},{6,7},{7,4},{8,9},{9,10},{10,1... | collective-permute-start | bytes 147464 | tf_op jit(solution)/shard_map/ppermute | solution.py:19
  94.3 32.5 %copy-start.2 = (f32[8,8,16,128]{3,2,1,0:T(8,128)S(1)}, f32[8,8,16,128]{3,2,1,0:T(8,128)}, u32[]{:S(2)}) copy-start(f32[8,8,16,128]{3,2,1,0:T(8,128)} %param.22) | copy-start | bytes 1572868
  94.5 6.7 %collective-permute-start.21 = (f32[1,4,16,128]{3,2,1,0:T(8,128)S(1)}, f32[1,4,16,128]{3,2,1,0:T(8,128)S(1)}, u32[]{:S(2)}, u32[]{:S(2)}) collective-permute-start(f32[1,4,16,128]{3,2,1,0:T(8,128)S(1)} %get-tuple-element.80), channel_id=1, source_target_pairs={{0,4},{4,8},{8,12},{12,16},{16,20},{20,24},{24,28},{28,0},{1,5},{5... | collective-permute-start | bytes 98312 | tf_op jit(solution)/shard_map/ppermute | solution.py:19
  94.6 6.7 %collective-permute-start.20 = (f32[1,4,16,128]{3,2,1,0:T(8,128)S(1)}, f32[1,4,16,128]{3,2,1,0:T(8,128)S(1)}, u32[]{:S(2)}, u32[]{:S(2)}) collective-permute-start(f32[1,4,16,128]{3,2,1,0:T(8,128)S(1)} %get-tuple-element.81), channel_id=1, source_target_pairs={{4,0},{8,4},{12,8},{16,12},{20,16},{24,20},{28,24},{0,28},{5,1},{9... | collective-permute-start | bytes 98312 | tf_op jit(solution)/shard_map/ppermute | solution.py:20
  101.3 1.8 %collective-permute-start.22 = (f32[6,1,16,128]{3,2,1,0:T(8,128)S(1)}, f32[6,1,16,128]{3,2,1,0:T(8,128)S(1)}, u32[]{:S(2)}, u32[]{:S(2)}) collective-permute-start(f32[6,1,16,128]{3,2,1,0:T(8,128)S(1)} %get-tuple-element.70), channel_id=1, source_target_pairs={{1,0},{2,1},{3,2},{0,3},{5,4},{6,5},{7,6},{4,7},{9,8},{10,9},{11,1... | collective-permute-start | bytes 147464 | tf_op jit(solution)/shard_map/ppermute | solution.py:20
  101.3 3.6 %collective-permute-start.23 = (f32[6,1,16,128]{3,2,1,0:T(8,128)S(1)}, f32[6,1,16,128]{3,2,1,0:T(8,128)S(1)}, u32[]{:S(2)}, u32[]{:S(2)}) collective-permute-start(f32[6,1,16,128]{3,2,1,0:T(8,128)S(1)} %get-tuple-element.71), channel_id=1, source_target_pairs={{0,1},{1,2},{2,3},{3,0},{4,5},{5,6},{6,7},{7,4},{8,9},{9,10},{10,1... | collective-permute-start | bytes 147464 | tf_op jit(solution)/shard_map/ppermute | solution.py:19
  105.1 6.7 %collective-permute-start.25 = (f32[1,4,16,128]{3,2,1,0:T(8,128)S(1)}, f32[1,4,16,128]{3,2,1,0:T(8,128)S(1)}, u32[]{:S(2)}, u32[]{:S(2)}) collective-permute-start(f32[1,4,16,128]{3,2,1,0:T(8,128)S(1)} %get-tuple-element.74), channel_id=1, source_target_pairs={{0,4},{4,8},{8,12},{12,16},{16,20},{20,24},{24,28},{28,0},{1,5},{5... | collective-permute-start | bytes 98312 | tf_op jit(solution)/shard_map/ppermute | solution.py:19
  105.1 6.7 %collective-permute-start.24 = (f32[1,4,16,128]{3,2,1,0:T(8,128)S(1)}, f32[1,4,16,128]{3,2,1,0:T(8,128)S(1)}, u32[]{:S(2)}, u32[]{:S(2)}) collective-permute-start(f32[1,4,16,128]{3,2,1,0:T(8,128)S(1)} %get-tuple-element.75), channel_id=1, source_target_pairs={{4,0},{8,4},{12,8},{16,12},{20,16},{24,20},{28,24},{0,28},{5,1},{9... | collective-permute-start | bytes 98312 | tf_op jit(solution)/shard_map/ppermute | solution.py:20
  111.8 1.8 %collective-permute-start.26 = (f32[6,1,16,128]{3,2,1,0:T(8,128)S(1)}, f32[6,1,16,128]{3,2,1,0:T(8,128)S(1)}, u32[]{:S(2)}, u32[]{:S(2)}) collective-permute-start(f32[6,1,16,128]{3,2,1,0:T(8,128)S(1)} %get-tuple-element.68), channel_id=1, source_target_pairs={{1,0},{2,1},{3,2},{0,3},{5,4},{6,5},{7,6},{4,7},{9,8},{10,9},{11,1... | collective-permute-start | bytes 147464 | tf_op jit(solution)/shard_map/ppermute | solution.py:20
  111.9 3.6 %collective-permute-start.27 = (f32[6,1,16,128]{3,2,1,0:T(8,128)S(1)}, f32[6,1,16,128]{3,2,1,0:T(8,128)S(1)}, u32[]{:S(2)}, u32[]{:S(2)}) collective-permute-start(f32[6,1,16,128]{3,2,1,0:T(8,128)S(1)} %get-tuple-element.69), channel_id=1, source_target_pairs={{0,1},{1,2},{2,3},{3,0},{4,5},{5,6},{6,7},{7,4},{8,9},{9,10},{10,1... | collective-permute-start | bytes 147464 | tf_op jit(solution)/shard_map/ppermute | solution.py:19
  116.3 6.5 %collective-permute-start.28 = (bf16[1,4,16,128]{3,2,1,0:T(8,128)(2,1)S(1)}, bf16[1,4,16,128]{3,2,1,0:T(8,128)(2,1)S(1)}, u32[]{:S(2)}, u32[]{:S(2)}) collective-permute-start(bf16[1,4,16,128]{3,2,1,0:T(8,128)(2,1)S(1)} %get-tuple-element.122), channel_id=1, source_target_pairs={{0,4},{4,8},{8,12},{12,16},{16,20},{20,24},{24,28},{28,0},{1,5},{5... | collective-permute-start | bytes 49160 | tf_op jit(solution)/shard_map/ppermute | solution.py:19
  116.3 6.5 %collective-permute-start.29 = (bf16[1,4,16,128]{3,2,1,0:T(8,128)(2,1)S(1)}, bf16[1,4,16,128]{3,2,1,0:T(8,128)(2,1)S(1)}, u32[]{:S(2)}, u32[]{:S(2)}) collective-permute-start(bf16[1,4,16,128]{3,2,1,0:T(8,128)(2,1)S(1)} %get-tuple-element.123), channel_id=1, source_target_pairs={{4,0},{8,4},{12,8},{16,12},{20,16},{24,20},{28,24},{0,28},{5,1},{9... | collective-permute-start | bytes 49160 | tf_op jit(solution)/shard_map/ppermute | solution.py:20
  122.8 3.3 %collective-permute-start.30 = (bf16[6,1,16,128]{3,2,1,0:T(8,128)(2,1)S(1)}, bf16[6,1,16,128]{3,2,1,0:T(8,128)(2,1)S(1)}, u32[]{:S(2)}, u32[]{:S(2)}) collective-permute-start(bf16[6,1,16,128]{3,2,1,0:T(8,128)(2,1)S(1)} %get-tuple-element.112), channel_id=1, source_target_pairs={{0,1},{1,2},{2,3},{3,0},{4,5},{5,6},{6,7},{7,4},{8,9},{9,10},{10,1... | collective-permute-start | bytes 73736 | tf_op jit(solution)/shard_map/ppermute | solution.py:19
  122.9 3.3 %collective-permute-start.31 = (bf16[6,1,16,128]{3,2,1,0:T(8,128)(2,1)S(1)}, bf16[6,1,16,128]{3,2,1,0:T(8,128)(2,1)S(1)}, u32[]{:S(2)}, u32[]{:S(2)}) collective-permute-start(bf16[6,1,16,128]{3,2,1,0:T(8,128)(2,1)S(1)} %get-tuple-element.113), channel_id=1, source_target_pairs={{1,0},{2,1},{3,2},{0,3},{5,4},{6,5},{7,6},{4,7},{9,8},{10,9},{11,1... | collective-permute-start | bytes 73736 | tf_op jit(solution)/shard_map/ppermute | solution.py:20
  126.9 16.0 %copy-start.1 = (f32[8,8,16,128]{3,2,1,0:T(8,128)S(1)}, f32[8,8,16,128]{3,2,1,0:T(8,128)}, u32[]{:S(2)}) copy-start(f32[8,8,16,128]{3,2,1,0:T(8,128)} %param.18) | copy-start | bytes 1572868
  130.4 7.3 %collective-permute-start.33 = (f32[1,8,16,128]{3,2,1,0:T(8,128)S(1)}, f32[1,8,16,128]{3,2,1,0:T(8,128)S(1)}, u32[]{:S(2)}, u32[]{:S(2)}) collective-permute-start(f32[1,8,16,128]{3,2,1,0:T(8,128)S(1)} %get-tuple-element.52), channel_id=1, source_target_pairs={{0,4},{4,8},{8,12},{12,16},{16,20},{20,24},{24,28},{28,0},{1,5},{5... | collective-permute-start | bytes 196616 | tf_op jit(solution)/shard_map/ppermute | solution.py:19
  130.4 7.3 %collective-permute-start.32 = (f32[1,8,16,128]{3,2,1,0:T(8,128)S(1)}, f32[1,8,16,128]{3,2,1,0:T(8,128)S(1)}, u32[]{:S(2)}, u32[]{:S(2)}) collective-permute-start(f32[1,8,16,128]{3,2,1,0:T(8,128)S(1)} %get-tuple-element.53), channel_id=1, source_target_pairs={{4,0},{8,4},{12,8},{16,12},{20,16},{24,20},{28,24},{0,28},{5,1},{9... | collective-permute-start | bytes 196616 | tf_op jit(solution)/shard_map/ppermute | solution.py:20
  137.7 3.2 %collective-permute-start.34 = (f32[10,1,16,128]{3,2,1,0:T(8,128)S(1)}, f32[10,1,16,128]{3,2,1,0:T(8,128)S(1)}, u32[]{:S(2)}, u32[]{:S(2)}) collective-permute-start(f32[10,1,16,128]{3,2,1,0:T(8,128)S(1)} %get-tuple-element.38), channel_id=1, source_target_pairs={{1,0},{2,1},{3,2},{0,3},{5,4},{6,5},{7,6},{4,7},{9,8},{10,9},{11,1... | collective-permute-start | bytes 245768 | tf_op jit(solution)/shard_map/ppermute | solution.py:20
  138.6 4.3 %collective-permute-start.35 = (f32[10,1,16,128]{3,2,1,0:T(8,128)S(1)}, f32[10,1,16,128]{3,2,1,0:T(8,128)S(1)}, u32[]{:S(2)}, u32[]{:S(2)}) collective-permute-start(f32[10,1,16,128]{3,2,1,0:T(8,128)S(1)} %get-tuple-element.39), channel_id=1, source_target_pairs={{0,1},{1,2},{2,3},{3,0},{4,5},{5,6},{6,7},{7,4},{8,9},{9,10},{10,1... | collective-permute-start | bytes 245768 | tf_op jit(solution)/shard_map/ppermute | solution.py:19
  143.4 7.3 %collective-permute-start.37 = (f32[1,8,16,128]{3,2,1,0:T(8,128)S(1)}, f32[1,8,16,128]{3,2,1,0:T(8,128)S(1)}, u32[]{:S(2)}, u32[]{:S(2)}) collective-permute-start(f32[1,8,16,128]{3,2,1,0:T(8,128)S(1)} %get-tuple-element.46), channel_id=1, source_target_pairs={{0,4},{4,8},{8,12},{12,16},{16,20},{20,24},{24,28},{28,0},{1,5},{5... | collective-permute-start | bytes 196616 | tf_op jit(solution)/shard_map/ppermute | solution.py:19
  143.4 7.2 %collective-permute-start.36 = (f32[1,8,16,128]{3,2,1,0:T(8,128)S(1)}, f32[1,8,16,128]{3,2,1,0:T(8,128)S(1)}, u32[]{:S(2)}, u32[]{:S(2)}) collective-permute-start(f32[1,8,16,128]{3,2,1,0:T(8,128)S(1)} %get-tuple-element.47), channel_id=1, source_target_pairs={{4,0},{8,4},{12,8},{16,12},{20,16},{24,20},{28,24},{0,28},{5,1},{9... | collective-permute-start | bytes 196616 | tf_op jit(solution)/shard_map/ppermute | solution.py:20
  150.7 2.5 %collective-permute-start.38 = (f32[10,1,16,128]{3,2,1,0:T(8,128)S(1)}, f32[10,1,16,128]{3,2,1,0:T(8,128)S(1)}, u32[]{:S(2)}, u32[]{:S(2)}) collective-permute-start(f32[10,1,16,128]{3,2,1,0:T(8,128)S(1)} %get-tuple-element.36), channel_id=1, source_target_pairs={{1,0},{2,1},{3,2},{0,3},{5,4},{6,5},{7,6},{4,7},{9,8},{10,9},{11,1... | collective-permute-start | bytes 245768 | tf_op jit(solution)/shard_map/ppermute | solution.py:20
  150.7 4.2 %collective-permute-start.39 = (f32[10,1,16,128]{3,2,1,0:T(8,128)S(1)}, f32[10,1,16,128]{3,2,1,0:T(8,128)S(1)}, u32[]{:S(2)}, u32[]{:S(2)}) collective-permute-start(f32[10,1,16,128]{3,2,1,0:T(8,128)S(1)} %get-tuple-element.37), channel_id=1, source_target_pairs={{0,1},{1,2},{2,3},{3,0},{4,5},{5,6},{6,7},{7,4},{8,9},{9,10},{10,1... | collective-permute-start | bytes 245768 | tf_op jit(solution)/shard_map/ppermute | solution.py:19
  155.5 7.1 %collective-permute-start.41 = (f32[1,8,16,128]{3,2,1,0:T(8,128)S(1)}, f32[1,8,16,128]{3,2,1,0:T(8,128)S(1)}, u32[]{:S(2)}, u32[]{:S(2)}) collective-permute-start(f32[1,8,16,128]{3,2,1,0:T(8,128)S(1)} %get-tuple-element.44), channel_id=1, source_target_pairs={{0,4},{4,8},{8,12},{12,16},{16,20},{20,24},{24,28},{28,0},{1,5},{5... | collective-permute-start | bytes 196616 | tf_op jit(solution)/shard_map/ppermute | solution.py:19
  155.5 7.0 %collective-permute-start.40 = (f32[1,8,16,128]{3,2,1,0:T(8,128)S(1)}, f32[1,8,16,128]{3,2,1,0:T(8,128)S(1)}, u32[]{:S(2)}, u32[]{:S(2)}) collective-permute-start(f32[1,8,16,128]{3,2,1,0:T(8,128)S(1)} %get-tuple-element.45), channel_id=1, source_target_pairs={{4,0},{8,4},{12,8},{16,12},{20,16},{24,20},{28,24},{0,28},{5,1},{9... | collective-permute-start | bytes 196616 | tf_op jit(solution)/shard_map/ppermute | solution.py:20
  162.6 2.3 %collective-permute-start.42 = (f32[10,1,16,128]{3,2,1,0:T(8,128)S(1)}, f32[10,1,16,128]{3,2,1,0:T(8,128)S(1)}, u32[]{:S(2)}, u32[]{:S(2)}) collective-permute-start(f32[10,1,16,128]{3,2,1,0:T(8,128)S(1)} %get-tuple-element.34), channel_id=1, source_target_pairs={{1,0},{2,1},{3,2},{0,3},{5,4},{6,5},{7,6},{4,7},{9,8},{10,9},{11,1... | collective-permute-start | bytes 245768 | tf_op jit(solution)/shard_map/ppermute | solution.py:20
  162.6 4.4 %collective-permute-start.43 = (f32[10,1,16,128]{3,2,1,0:T(8,128)S(1)}, f32[10,1,16,128]{3,2,1,0:T(8,128)S(1)}, u32[]{:S(2)}, u32[]{:S(2)}) collective-permute-start(f32[10,1,16,128]{3,2,1,0:T(8,128)S(1)} %get-tuple-element.35), channel_id=1, source_target_pairs={{0,1},{1,2},{2,3},{3,0},{4,5},{5,6},{6,7},{7,4},{8,9},{9,10},{10,1... | collective-permute-start | bytes 245768 | tf_op jit(solution)/shard_map/ppermute | solution.py:19
